TPU v7x, 32 devices: a whole 2x2x4 slice. The times are simulated.
32 devices in a mesh: dp: 8 (over y, x, core), tensor: 4 (over z).
Axes of the slice: x: 2, y: 2, z: 4, core: 2. Of those that a mesh axis runs over, the one named last changes fastest.
Arguments:
- tokens: bfloat16 [32, 256, 1152], P(('dp', 'tensor')), may hold values from -6 to 6
- timesteps: int32 [32], P('dp'), may hold values from 0 to 999
- labels: int32 [32], P('dp'), may hold values from 0 to 999
- item_counts: int32 [8], P('dp'), may hold values from 1 to 4
- cotangent: bfloat16 [32, 256, 1152], P(('dp', 'tensor')), may hold values from -6 to 6
- project_weight: bfloat16 [1152, 3, 1152], P(None, None, 'tensor'), may hold values from -0.1875 to 0.1875
- query_gain: bfloat16 [72], replicated, may hold values from 0.099609375 to 1.8984375
- key_gain: bfloat16 [72], replicated, may hold values from 0.099609375 to 1.8984375
- output_weight: bfloat16 [1152, 1152], P('tensor'), may hold values from -0.5 to 0.5
- output_bias: bfloat16 [1152], replicated, may hold values from -3 to 3
- expand_weight: bfloat16 [1152, 2, 3072], P(None, None, 'tensor'), may hold values from -0.1875 to 0.1875
- down_weight: bfloat16 [3072, 1152], P('tensor'), may hold values from -0.15625 to 0.15625
- down_bias: bfloat16 [1152], replicated, may hold values from -3 to 3
- modulate_weight: bfloat16 [1152, 6, 1152], P(None, None, 'tensor'), may hold values from -0.1875 to 0.1875
- modulate_bias: bfloat16 [6, 1152], P(None, 'tensor'), may hold values from -3 to 3
- time_weight: bfloat16 [256, 1152], replicated, may hold values from -0.5 to 0.5
- time_bias: bfloat16 [1152], replicated, may hold values from -3 to 3
- embed_weight: bfloat16 [1152, 1152], replicated, may hold values from -0.25 to 0.25
- embed_bias: bfloat16 [1152], replicated, may hold values from -3 to 3
- class_table: bfloat16 [1000, 1152], replicated, may hold values from -6 to 6
Outputs:
- result: bfloat16 [32, 256, 1152], P(('dp', 'tensor'))
- tokens_grad: bfloat16 [32, 256, 1152], P(('dp', 'tensor'))
- project_grad: float32 [1152, 3, 1152], P('dp', None, 'tensor')
- query_gain_grad: float32 [72], replicated
- key_gain_grad: float32 [72], replicated
- output_weight_grad: float32 [1152, 1152], P('tensor', 'dp')
- output_bias_grad: float32 [1152], replicated
- expand_grad: float32 [1152, 2, 3072], P('dp', None, 'tensor')
- down_grad: float32 [3072, 1152], P('tensor', 'dp')
- down_bias_grad: float32 [1152], replicated
- modulate_grad: float32 [1152, 6, 1152], P('dp', None, 'tensor')
- modulate_bias_grad: float32 [6, 1152], replicated
- time_grad: float32 [256, 1152], P(None, 'dp')
- time_bias_grad: float32 [1152], P('dp')
- embed_grad: float32 [1152, 1152], P('dp')
- embed_bias_grad: float32 [1152], P('dp')
- class_grad: float32 [1000, 1152], P(None, 'dp')
Inputs may be any that keep to these rules, and one draw needn't show every extreme that they name: `item_counts`: entry i counts the real items among the 4 items of index i of dp; they are its first ones.
All inputs are finite; a program needn't handle non-finite values.
Results may differ from a plain program's by a relative error of at most 0.03.
Values may be sent and summed in bfloat16 or wider, within the bound.
A program may use at most 256 MiB of HBM per device.

v0:
```python
import functools
import math

import jax
import jax.numpy as jnp
from jax import lax
from jax.experimental import pallas as pl
from jax.experimental.pallas import tpu as pltpu
from jax.sharding import PartitionSpec as P

HD = 72
FREQ = 256
GRID = 16


EPS = 1e-06


def layer_norm(value):
    center = value - jnp.mean(value, axis=-1, keepdims=True)
    inverse = lax.rsqrt(jnp.mean(center * center, axis=-1, keepdims=True) + EPS)
    return (center * inverse, inverse)


def layer_norm_back(normed, inverse, grad):
    return inverse * (
        grad
        - jnp.mean(grad, axis=-1, keepdims=True)
        - normed * jnp.mean(grad * normed, axis=-1, keepdims=True)
    )


def silu_slope(value):
    sigma = jax.nn.sigmoid(value)
    return sigma * (1.0 + value * (1.0 - sigma))


def rotate(value, positions):
    quarter = HD // 4
    rates = 10000.0 ** (-jnp.arange(quarter, dtype=jnp.float32) / quarter)
    places = ((positions // GRID).astype(jnp.float32), (positions % GRID).astype(jnp.float32))
    pieces = []
    for which_half in range(2):
        half_value = value[..., which_half * 2 * quarter : (which_half + 1) * 2 * quarter]
        angle = places[which_half][:, None] * rates[None, :]
        cosine = jnp.cos(angle)[None, :, None, :]
        sine = jnp.sin(angle)[None, :, None, :]
        first = half_value[..., :quarter]
        second = half_value[..., quarter:]
        pieces.append(first * cosine - second * sine)
        pieces.append(second * cosine + first * sine)
    return jnp.concatenate(pieces, axis=-1)


def head_prepare(raw, gain, positions):
    scaled = raw * lax.rsqrt(jnp.mean(raw * raw, axis=-1, keepdims=True) + EPS) * gain
    return rotate(scaled, positions)


def time_features(steps_in):
    half = FREQ // 2
    rates = jnp.exp(-math.log(10000.0) * jnp.arange(half, dtype=jnp.float32) / half)
    angle = steps_in.astype(jnp.float32)[:, None] * rates[None, :]
    return jnp.concatenate([jnp.cos(angle), jnp.sin(angle)], axis=-1)


CHUNKS = 8


def rows_of(block, total):
    size = total // CHUNKS
    return pl.ds(pl.multiple_of(block * size, size), size)


class Line:
    def __init__(self, count, gathered, summed, ag_sems, rs_sems):
        self.count = count
        self.place = lax.axis_index("tensor")
        self.gathered = gathered
        self.summed = summed
        self.ag_send, self.ag_recv = ag_sems
        self.rs_send, self.rs_recv = rs_sems

    def barrier(self, wide=1):
        place, count = self.place, self.count
        sem = pltpu.get_barrier_semaphore()

        @pl.when(place > 0)
        def _():
            pl.semaphore_signal(sem, inc=1, device_id={"tensor": place - 1})

        @pl.when(place < count - 1)
        def _():
            pl.semaphore_signal(sem, inc=1, device_id={"tensor": place + 1})

        peers = jnp.where(place > 0, 1, 0) + jnp.where(place < count - 1, 1, 0)
        here = lax.axis_index("dp")

        @pl.loop(1, wide)
        def _(offset):
            peer = lax.rem(here + offset, wide)
            pl.semaphore_signal(sem, inc=1, device_id={"dp": peer})

        pl.semaphore_wait(sem, peers + (wide - 1))

    def item_copy(self, which, way, item, own=False):
        mine, everyone = self.gathered[which]
        target = self.place + (1 if way == 0 else -1)
        return pltpu.make_async_remote_copy(
            src_ref=mine if own else everyone.at[item],
            dst_ref=everyone.at[item],
            send_sem=self.ag_send.at[which, way, item],
            recv_sem=self.ag_recv.at[which, way, item],
            device_id={"tensor": target},
        )

    def can(self, way):
        return self.place < self.count - 1 if way == 0 else self.place > 0

    def sum_copy(self, which, way, item, block):
        part, landed = self.summed[which]
        target = self.place + (1 if way == 0 else -1)
        slot = item
        if way == 1:
            slot = jnp.where(item == target, self.count, item)
        rows = rows_of(block, part.shape[1])
        return pltpu.make_async_remote_copy(
            src_ref=part.at[item, rows],
            dst_ref=landed.at[slot, rows],
            send_sem=self.rs_send.at[which, way, item, block],
            recv_sem=self.rs_recv.at[which, way, item, block],
            device_id={"tensor": target},
        )

    def landed_slot(self, way, item):
        return jnp.where(item == self.place, self.count, item) if way == 1 else item

    def wait_sum(self, which, way, item, block):
        part, landed = self.summed[which]
        rows = rows_of(block, part.shape[1])
        view = landed.at[self.landed_slot(way, item), rows]
        pltpu.make_async_remote_copy(
            src_ref=view,
            dst_ref=view,
            send_sem=self.rs_send.at[which, way, item, block],
            recv_sem=self.rs_recv.at[which, way, item, block],
            device_id={"tensor": self.place},
        ).wait_recv()
        return view

    def start_own(self):
        for which in range(len(self.gathered)):
            for way in range(2):

                @pl.when(self.can(way))
                def _():
                    self.item_copy(which, way, self.place, own=True).start()

    def receive(self, step):
        place, count = self.place, self.count
        for which in range(len(self.gathered)):
            for way in range(2):
                item = place - step if way == 0 else place + step

                @pl.when((item >= 0) & (item < count))
                def _():
                    self.item_copy(which, way, item).wait_recv()

                    @pl.when(self.can(way))
                    def _():
                        self.item_copy(which, way, item).start()

    def items(self, step):
        place, count = self.place, self.count
        low, high = place - step, place + step
        return ((low, (low >= 0)), (high, (high < count) & (step > 0)))

    def moves(self, step):
        place, count = self.place, self.count
        return (
            (0, step, step > place, place),
            (1, count - 1 - step, count - 1 - step < place, count - 1 - place),
        )

    def first_sums(self, step, arrays=(0,)):
        @pl.loop(0, CHUNKS)
        def _(block):
            for way, item, further, hop in self.moves(step):

                @pl.when(further & (hop == 0))
                def _():
                    for which in arrays:
                        self.sum_copy(which, way, item, block).start()

    def relay_sums(self, step, arrays=(0,)):
        @pl.loop(0, CHUNKS + self.count - 3)
        def _(turn):
            for distance in range(1, self.count - 1):
                block = turn - (distance - 1)
                for way, item, further, hop in self.moves(step):

                    @pl.when(further & (hop == distance) & (block >= 0) & (block < CHUNKS))
                    def _():
                        for which in arrays:
                            part, landed = self.summed[which]
                            rows = rows_of(block, part.shape[1])
                            view = self.wait_sum(which, way, item, block)
                            total = part[item, rows].astype(jnp.float32) + view[...].astype(
                                jnp.float32
                            )
                            part[item, rows] = total.astype(part.dtype)
                            self.sum_copy(which, way, item, block).start()

    def each(self, first, second, body):
        @pl.loop(0, 2)
        def _(turn):
            item = jnp.where(turn == 0, first[0], second[0])
            valid = ((turn == 0) & first[1]) | ((turn == 1) & second[1])

            @pl.when(valid)
            def _():
                body(item)

    def near(self, step):
        place, count = self.place, self.count
        low = place >= step
        return jnp.where(low, place - step, place + step), low | (place + step < count)

    def far(self, step):
        place, count = self.place, self.count
        return place + step, (step > 0) & (place >= step) & (place + step < count)

    def finish(self, which, out):
        place, count = self.place, self.count
        part, landed = self.summed[which]

        @pl.loop(0, CHUNKS)
        def _(block):
            rows = rows_of(block, part.shape[1])
            out[rows] = part[place, rows].astype(jnp.float32)
            for way in range(2):

                @pl.when(place > 0 if way == 0 else place < count - 1)
                def _():
                    view = self.wait_sum(which, way, place, block)
                    out[rows] += view[...].astype(jnp.float32)

    def drain(self):
        place, count = self.place, self.count

        @pl.loop(0, count)
        def _(item):
            for way in range(2):
                passed = item <= place if way == 0 else item >= place

                @pl.when(passed & self.can(way))
                def _():
                    for which in range(len(self.gathered)):
                        self.item_copy(which, way, item).wait_send()

                further = item > place if way == 0 else item < place

                @pl.when(further)
                def _():
                    @pl.loop(0, CHUNKS)
                    def _(block):
                        for which in range(len(self.summed)):
                            self.sum_copy(which, way, item, block).wait_send()


def dot(left, right):
    return jnp.dot(left, right, preferred_element_type=jnp.float32)


def dot_rt(left, right):
    return lax.dot_general(
        left, right, (((1,), (1,)), ((), ())), preferred_element_type=jnp.float32
    )


def dot_lt(left, right):
    return lax.dot_general(
        left, right, (((0,), (0,)), ((), ())), preferred_element_type=jnp.float32
    )


def cut(total, most):
    size = max(s for s in range(128, most + 1, 128) if total % s == 0)
    return size, total // size


def span(index, size):
    return pl.ds(pl.multiple_of(index * size, size), size)


def feed_kernel(
    count,
    mod_ref,
    grad_ref,
    expand_hbm,
    down_hbm,
    feed_out,
    back_out,
    weight_hbm,
    expand,
    down,
    mod_all,
    grad_all,
    hidden,
    slopes,
    feed_part,
    back_part,
    feed_land,
    back_land,
    total,
    weights,
    load_sem,
    ag_send,
    ag_recv,
    rs_send,
    rs_recv,
):
    line = Line(
        count,
        [(mod_ref, mod_all), (grad_ref, grad_all)],
        [(back_part, back_land), (feed_part, feed_land)],
        (ag_send, ag_recv),
        (rs_send, rs_recv),
    )
    width, units = expand.shape[1], expand.shape[2]
    loads = (
        pltpu.make_async_copy(expand_hbm, expand, load_sem.at[0]),
        pltpu.make_async_copy(down_hbm, down, load_sem.at[1]),
    )
    for load in loads:
        load.start()
    line.barrier()
    line.start_own()
    mod_all[line.place] = mod_ref[...]
    grad_all[line.place] = grad_ref[...]
    total[...] = jnp.zeros_like(total)
    for load in loads:
        load.wait()
    unit_size, unit_count = cut(units, 256)
    wide_size, wide_count = cut(width, 384)
    tall_size, tall_count = cut(width, 128)

    def compute(item):
        @pl.loop(0, unit_count)
        def _(index):
            cols = span(index, unit_size)
            mod = mod_all[item]
            gate = dot(mod, expand[0, :, cols])
            upper = dot(mod, expand[1, :, cols])
            back = dot_rt(grad_all[item], down[cols, :])
            sigma = jax.nn.sigmoid(gate)
            active = gate * sigma
            hidden[item, :, cols] = (active * upper).astype(jnp.bfloat16)
            slopes[0, item, :, cols] = (
                back * upper * (sigma * (1.0 + gate * (1.0 - sigma)))
            ).astype(jnp.bfloat16)
            slopes[1, item, :, cols] = (back * active).astype(jnp.bfloat16)

        @pl.loop(0, wide_count)
        def _(index):
            cols = span(index, wide_size)
            back_part[item, :, cols] = (
                dot_rt(slopes[0, item], expand[0, cols, :])
                + dot_rt(slopes[1, item], expand[1, cols, :])
            ).astype(jnp.bfloat16)
            feed_part[item, :, cols] = dot(hidden[item], down[:, cols]).astype(jnp.bfloat16)

    def weigh(item):
        @pl.loop(0, tall_count)
        def _(index):
            rows = span(index, tall_size)
            mod = mod_all[item, :, rows]
            total[0, rows, :] += dot_lt(mod, slopes[0, item])
            total[1, rows, :] += dot_lt(mod, slopes[1, item])
            total[2, rows, :] += dot_lt(grad_all[item, :, rows], hidden[item])

    @pl.loop(0, count)
    def _(step):
        @pl.when(step > 0)
        def _():
            line.each(line.far(step - 1), line.near(step - 1), weigh)
            line.receive(step)

        line.each(line.far(step), line.near(step), compute)

        @pl.when(step > 0)
        def _():
            line.first_sums(step, (0, 1))
            line.relay_sums(step, (0, 1))

    line.each((0, False), line.near(count - 1), weigh)
    weights[...] = total[...].astype(jnp.bfloat16)
    store = pltpu.make_async_copy(weights, weight_hbm, load_sem.at[0])
    store.start()
    line.finish(0, back_out)
    line.finish(1, feed_out)
    line.drain()
    store.wait()


def feed_pass(mod_two, branch_grad, expand_weight, down_weight):
    count = lax.axis_size("tensor")
    length, width = mod_two.shape
    units = down_weight.shape[0]
    expand = jnp.transpose(expand_weight, (1, 0, 2))
    vmem, any_space = pl.BlockSpec(memory_space=pltpu.VMEM), pl.BlockSpec(memory_space=pl.ANY)
    low = jnp.bfloat16
    item = (length, width)
    return pl.pallas_call(
        functools.partial(feed_kernel, count),
        out_shape=(
            jax.ShapeDtypeStruct(item, jnp.float32),
            jax.ShapeDtypeStruct(item, jnp.float32),
            jax.ShapeDtypeStruct((3, width, units), low),
        ),
        in_specs=[vmem, vmem, any_space, any_space],
        out_specs=(vmem, vmem, any_space),
        scratch_shapes=[
            pltpu.VMEM((2, width, units), low),
            pltpu.VMEM((units, width), low),
            pltpu.VMEM((count, *item), low),
            pltpu.VMEM((count, *item), low),
            pltpu.VMEM((count, length, units), low),
            pltpu.VMEM((2, count, length, units), low),
            pltpu.VMEM((count, *item), low),
            pltpu.VMEM((count, *item), low),
            pltpu.VMEM((count + 1, *item), low),
            pltpu.VMEM((count + 1, *item), low),
            pltpu.VMEM((3, width, units), jnp.float32),
            pltpu.VMEM((3, width, units), low),
            *line_sems(count, 2, 2),
        ],
        compiler_params=pltpu.CompilerParams(
            collective_id=1, has_side_effects=True, vmem_limit_bytes=64000000
        ),
        name="feed_pass",
    )(mod_two, branch_grad, expand, down_weight)


def swap_kernel(jobs, total, *refs):
    n = len(jobs)
    ins, outs = refs[:n], refs[n + total : 2 * n + total]
    sems = refs[2 * n + 2 * total :]
    places = [lax.axis_index(axis) for axis, _, _ in jobs]
    hello = pltpu.get_barrier_semaphore()
    axes = []
    for axis, count, _ in jobs:
        if (axis, count) not in axes:
            axes.append((axis, count))
    if total:
        axes = [("dp", lax.axis_size("dp")), ("tensor", lax.axis_size("tensor"))]
    for axis, count in axes:
        here = lax.axis_index(axis)

        @pl.loop(1, count)
        def _(offset):
            peer = lax.rem(here + offset, count)
            pl.semaphore_signal(hello, inc=1, device_id={axis: peer})

    pl.semaphore_wait(hello, sum(count - 1 for _, count in axes))

    def copy(source, target, send, recv, axis, peer, slot):
        return pltpu.make_async_remote_copy(
            src_ref=source,
            dst_ref=target.at[slot],
            send_sem=send.at[peer],
            recv_sem=recv.at[slot],
            device_id={axis: peer},
        )

    def start(source, target, send, recv, axis, count, split):
        here = lax.axis_index(axis)

        @pl.loop(1, count)
        def _(offset):
            peer = lax.rem(here + offset, count)
            piece = source.at[peer] if split else source
            copy(piece, target, send, recv, axis, peer, here).start()

        target[here] = source[here] if split else source[...]

    def finish(source, target, send, recv, axis, count, split):
        here = lax.axis_index(axis)

        @pl.loop(1, count)
        def _(offset):
            peer = lax.rem(here + offset, count)
            piece = source.at[peer] if split else source
            step = copy(piece, target, send, recv, axis, peer, peer)
            step.wait_recv()
            step.wait_send()

    work = []
    for index, (axis, count, split) in enumerate(jobs):
        work.append((ins[index], outs[index], sems[2 * index], sems[2 * index + 1], axis, count, split))
    if total:
        source, result = refs[n], refs[2 * n + total]
        one, two, middle, s1, r1, s2, r2 = sems[2 * n :]
        wide, deep = lax.axis_size("dp"), lax.axis_size("tensor")
        first = (source, one, s1, r1, "dp", wide, False)
        start(*first)
    for job in work:
        start(*job)
    if total:
        finish(*first)
        middle[...] = one[0]

        @pl.loop(1, wide)
        def _(index):
            middle[...] += one[index]

        second = (middle, two, s2, r2, "tensor", deep, False)
        start(*second)
    for job in work:
        finish(*job)
    if total:
        finish(*second)
        result[...] = two[0]

        @pl.loop(1, deep)
        def _(index):
            result[...] += two[index]


def swap(name, number, jobs, total=None):
    vmem = pl.BlockSpec(memory_space=pltpu.VMEM)
    plan, arrays, shapes, scratch = [], [], [], []
    for array, axis, split in jobs:
        count = lax.axis_size(axis)
        plan.append((axis, count, split))
        arrays.append(array)
        piece = array.shape[1:] if split else array.shape
        shapes.append(jax.ShapeDtypeStruct((count, *piece), array.dtype))
        scratch += [pltpu.SemaphoreType.DMA((count,)), pltpu.SemaphoreType.DMA((count,))]
    if total is not None:
        wide, deep = lax.axis_size("dp"), lax.axis_size("tensor")
        arrays.append(total)
        shapes.append(jax.ShapeDtypeStruct(total.shape, total.dtype))
        scratch += [
            pltpu.VMEM((wide, *total.shape), total.dtype),
            pltpu.VMEM((deep, *total.shape), total.dtype),
            pltpu.VMEM(total.shape, total.dtype),
        ]
        for count in (wide, wide, deep, deep):
            scratch.append(pltpu.SemaphoreType.DMA((count,)))
    return pl.pallas_call(
        functools.partial(swap_kernel, tuple(plan), int(total is not None)),
        out_shape=tuple(shapes),
        in_specs=[vmem] * len(arrays),
        out_specs=tuple([vmem] * len(shapes)),
        scratch_shapes=scratch,
        compiler_params=pltpu.CompilerParams(collective_id=number, has_side_effects=True),
        name=name,
    )(*arrays)


LANES = 128
HEAD_UNROLL = 2


def turn(value, tables):
    return (
        value * tables[0]
        + pltpu.roll(value, LANES - HD // 4, 1) * tables[1]
        + pltpu.roll(value, HD // 4, 1) * tables[2]
    )


def turn_back(grad, tables):
    return (
        grad * tables[0]
        + pltpu.roll(grad * tables[1], HD // 4, 1)
        + pltpu.roll(grad * tables[2], LANES - HD // 4, 1)
    )


def turn_tables(length):
    quarter = HD // 4
    lane = jnp.arange(LANES)
    rates = 10000.0 ** (-(lane % quarter).astype(jnp.float32) / quarter)
    positions = jnp.arange(length)[:, None]
    place = jnp.where(lane < 2 * quarter, positions // GRID, positions % GRID)
    angle = place.astype(jnp.float32) * rates
    real = lane < HD
    early = (lane // quarter) % 2 == 0
    cosine = jnp.where(real, jnp.cos(angle), 0.0)
    sine = jnp.sin(angle)
    return jnp.stack(
        [
            cosine,
            jnp.where(real & early, -sine, 0.0),
            jnp.where(real & ~early, sine, 0.0),
        ]
    )


def unit_norm(raw):
    inverse = lax.rsqrt(jnp.sum(raw * raw, axis=-1, keepdims=True) * (1.0 / HD) + EPS)
    return raw * inverse, inverse


def project(mod, weight, raw):
    @pl.loop(0, weight.shape[0])
    def _(index):
        raw[index] = dot(mod, weight[index])


def soft(queries, keys):
    grown = jnp.exp2(dot_rt(queries, keys) * (HD ** (-0.5) / math.log(2.0)))
    return grown * (1.0 / jnp.sum(grown, axis=-1, keepdims=True))


def attend_kernel(
    count,
    mod_ref,
    tables_ref,
    gains_ref,
    weight_hbm,
    last_hbm,
    branch_out,
    mod_out,
    weight,
    last,
    mod_all,
    raw,
    mixed,
    part,
    land,
    load_sem,
    ag_send,
    ag_recv,
    rs_send,
    rs_recv,
):
    line = Line(count, [(mod_ref, mod_all)], [(part, land)], (ag_send, ag_recv), (rs_send, rs_recv))
    loads = (
        pltpu.make_async_copy(weight_hbm, weight, load_sem.at[0]),
        pltpu.make_async_copy(last_hbm, last, load_sem.at[1]),
    )
    for load in loads:
        load.start()
    line.barrier()
    line.start_own()
    mod_all[line.place] = mod_ref[...]
    for load in loads:
        load.wait()
    heads = last.shape[0] // LANES
    wide_size, wide_count = cut(last.shape[1], 384)

    def compute(item):
        project(mod_all[item], weight, raw)
        tables = (tables_ref[0], tables_ref[1], tables_ref[2])

        @pl.loop(0, heads, unroll=HEAD_UNROLL)
        def _(head):
            lanes = span(head, LANES)
            queries = turn(unit_norm(raw[0, :, lanes])[0] * gains_ref[0:1, :], tables)
            keys = turn(unit_norm(raw[1, :, lanes])[0] * gains_ref[1:2, :], tables)
            probs = soft(queries.astype(jnp.bfloat16), keys.astype(jnp.bfloat16))
            values = raw[2, :, lanes].astype(jnp.bfloat16)
            mixed[:, lanes] = dot(probs.astype(jnp.bfloat16), values).astype(jnp.bfloat16)

        @pl.loop(0, wide_count)
        def _(index):
            cols = span(index, wide_size)
            part[item, :, cols] = dot(mixed[...], last[:, cols]).astype(jnp.bfloat16)

    @pl.loop(0, count)
    def _(step):
        @pl.when(step > 0)
        def _():
            line.receive(step)

        line.each(line.far(step - 1), line.near(step), compute)

        @pl.when(step > 0)
        def _():
            line.first_sums(step)
            line.relay_sums(step)

    mod_out[...] = mod_all[...]
    line.finish(0, branch_out)
    line.drain()


def block_copy(array, target, slot, block, size, send, recv, peer):
    rows = pl.ds(pl.multiple_of(block * size, size), size)
    source = array.at[rows] if len(array.shape) == 2 else array.at[:, rows]
    return pltpu.make_async_remote_copy(
        src_ref=source,
        dst_ref=target.at[slot],
        send_sem=send,
        recv_sem=recv,
        device_id={"dp": peer},
    )


def attend_back_kernel(
    count,
    wide,
    grad_ref,
    mod_all,
    tables_ref,
    gains_ref,
    narrow_ref,
    weight_hbm,
    last_hbm,
    *rest,
):
    if wide:
        feed_hbm, back_out, weight_out, gain_out, feed_out, *rest = rest
    else:
        back_out, weight_out, gain_out, *rest = rest
    (
        weight,
        last,
        grad_all,
        raw,
        mixed,
        mixed_grad,
        raw_grad,
        kept,
        kept_mixed,
        part,
        land,
        total,
        load_sem,
        ag_send,
        ag_recv,
        rs_send,
        rs_recv,
        *rest,
    ) = rest
    line = Line(count, [(grad_ref, grad_all)], [(part, land)], (ag_send, ag_recv), (rs_send, rs_recv))
    loads = (
        pltpu.make_async_copy(weight_hbm, weight, load_sem.at[0]),
        pltpu.make_async_copy(last_hbm, last, load_sem.at[1]),
    )
    for load in loads:
        load.start()
    line.barrier(wide or 1)
    line.start_own()
    width = last.shape[1]
    here = lax.axis_index("dp")
    if wide:
        feed_land, staged, pair_land, quad_land, fs, fr, ps, pr, qs, qr = rest
        size = width // wide
        half = wide // 2
        parity, seat = lax.rem(here, 2), here // 2
        partner = here + 1 - 2 * parity

        def feed_copy(peer, slot):
            return block_copy(feed_hbm, feed_land, slot, peer, size, fs.at[peer], fr.at[slot], peer)

        def pair_copy(index):
            block = 2 * index + 1 - parity
            return block_copy(
                staged, pair_land, index, block, size, ps.at[index], pr.at[index], partner
            )

        def quad_copy(index, slot):
            block = 2 * index + parity
            return block_copy(
                staged, quad_land, slot, block, size, qs.at[index], qr.at[slot], block
            )

        @pl.loop(1, wide)
        def _(offset):
            peer = lax.rem(here + offset, wide)
            feed_copy(peer, here).start()

    grad_all[line.place] = grad_ref[...]
    total[...] = jnp.zeros_like(total)
    gain_out[...] = jnp.zeros_like(gain_out)
    for load in loads:
        load.wait()
    inner = last.shape[0]
    heads = inner // LANES
    scale = HD ** (-0.5)
    wide_size, wide_count = cut(width, 384)
    inner_size, inner_count = cut(inner, 256)
    tall_size, tall_count = cut(width, 128)
    first_width = kept.shape[2]

    def compute(item):
        project(mod_all[item], weight, raw)
        tables = (tables_ref[0], tables_ref[1], tables_ref[2])

        @pl.loop(0, inner_count)
        def _(index):
            cols = span(index, inner_size)
            mixed_grad[:, cols] = dot_rt(grad_all[item], last[cols, :]).astype(jnp.bfloat16)

        @pl.loop(0, heads, unroll=HEAD_UNROLL)
        def _(head):
            lanes = span(head, LANES)
            query_norm, query_inverse = unit_norm(raw[0, :, lanes])
            key_norm, key_inverse = unit_norm(raw[1, :, lanes])
            values = raw[2, :, lanes].astype(jnp.bfloat16)
            queries = turn(query_norm * gains_ref[0:1, :], tables).astype(jnp.bfloat16)
            keys = turn(key_norm * gains_ref[1:2, :], tables).astype(jnp.bfloat16)
            probs = soft(queries, keys)
            probs_low = probs.astype(jnp.bfloat16)
            mixed[:, lanes] = dot(probs_low, values).astype(jnp.bfloat16)
            grad = mixed_grad[:, lanes]
            prob_grad = dot_rt(grad, values)
            score_grad = (
                probs * (prob_grad - jnp.sum(probs * prob_grad, axis=-1, keepdims=True))
            ).astype(jnp.bfloat16)

            def back(which, value_grad, norm, inverse):
                turned = turn_back(value_grad, tables)
                gained = turned * norm
                gain_out[which] += jnp.sum(gained.reshape(-1, 8, LANES), axis=0)
                scaled = turned * gains_ref[which : which + 1, :]
                mean = jnp.sum(scaled * norm, axis=-1, keepdims=True) * (1.0 / HD)
                raw_grad[which, :, lanes] = (inverse * (scaled - norm * mean)).astype(
                    jnp.bfloat16
                )

            back(0, dot(score_grad, keys) * scale, query_norm, query_inverse)
            back(1, dot_lt(score_grad, queries) * scale, key_norm, key_inverse)
            raw_grad[2, :, lanes] = dot_lt(probs_low, grad).astype(jnp.bfloat16)

        @pl.loop(0, wide_count)
        def _(index):
            cols = span(index, wide_size)
            sums = dot_rt(raw_grad[0], weight[0, cols, :])
            sums += dot_rt(raw_grad[1], weight[1, cols, :])
            sums += dot_rt(raw_grad[2], weight[2, cols, :])
            part[item, :, cols] = sums.astype(jnp.bfloat16)

    def keep(item):
        one = dot(raw_grad[0], narrow_ref[0])
        two = dot(raw_grad[1], narrow_ref[1])
        three = dot(raw_grad[2], narrow_ref[2])
        side = one.shape[1] - LANES
        low = jnp.bfloat16
        kept[item, :, :side] = one[:, :side].astype(low)
        kept[item, :, side : side + LANES] = (one[:, side:] + two[:, :LANES]).astype(low)
        kept[item, :, side + LANES : 2 * side] = two[:, LANES:side].astype(low)
        kept[item, :, 2 * side : 2 * side + LANES] = (two[:, side:] + three[:, :LANES]).astype(low)
        kept[item, :, 2 * side + LANES :] = three[:, LANES:].astype(low)
        kept_mixed[item] = dot(mixed[...], narrow_ref[0]).astype(low)

    def weigh(item):
        @pl.loop(0, tall_count)
        def _(index):
            rows = span(index, tall_size)
            total[rows, :first_width] += dot_lt(mod_all[item, :, rows], kept[item])
            total[rows, first_width:] += dot_lt(grad_all[item, :, rows], kept_mixed[item])

    def work(item):
        compute(item)
        keep(item)

    @pl.loop(0, count)
    def _(step):
        @pl.when(step > 0)
        def _():
            line.each(line.far(step - 2), line.near(step - 1), weigh)
            line.receive(step)

        line.each(line.far(step - 1), line.near(step), work)

        @pl.when(step > 0)
        def _():
            line.first_sums(step)

        @pl.when(step == count - 1)
        def _():
            line.each((0, False), line.near(step), weigh)
            if wide:
                staged[...] = total[...].astype(jnp.bfloat16)

                @pl.loop(0, half)
                def _(index):
                    pair_copy(index).start()

                @pl.loop(0, half)
                def _(index):
                    pair_copy(index).wait_send()
                    pair_copy(index).wait_recv()
                    rows = pl.ds(pl.multiple_of((2 * index + parity) * size, size), size)
                    staged[rows] = (
                        staged[rows].astype(jnp.float32) + pair_land[index].astype(jnp.float32)
                    ).astype(jnp.bfloat16)

                @pl.loop(1, half)
                def _(offset):
                    quad_copy(lax.rem(seat + offset, half), seat).start()

        @pl.when(step > 0)
        def _():
            line.relay_sums(step)

    if wide:
        rows = pl.ds(pl.multiple_of(here * size, size), size)
        own = pltpu.make_async_copy(feed_hbm.at[:, rows], feed_land.at[here], load_sem.at[0])
        own.start()

        @pl.loop(1, wide)
        def _(offset):
            peer = lax.rem(here + offset, wide)
            feed_copy(peer, here).wait_send()
            feed_copy(here, peer).wait_recv()

        own.wait()
        for which in range(feed_out.shape[0]):
            total_here = feed_land[0, which].astype(jnp.float32)
            for index in range(1, wide):
                total_here += feed_land[index, which].astype(jnp.float32)
            feed_out[which] = total_here

    line.finish(0, back_out)
    line.drain()
    if wide:
        weight_out[...] = staged[rows].astype(jnp.float32)

        @pl.loop(1, half)
        def _(offset):
            index = lax.rem(seat + offset, half)
            quad_copy(index, seat).wait_send()
            quad_copy(seat, index).wait_recv()
            weight_out[...] += quad_land[index].astype(jnp.float32)

    else:
        weight_out[...] = total[...].astype(jnp.bfloat16)


def attend_arrays(project_weight, output_weight, query_gain, key_gain, length):
    inner = project_weight.shape[2]
    heads = inner // HD
    low = jnp.bfloat16
    spot = jnp.arange(heads * LANES)
    real = spot % LANES < HD
    column = spot // LANES * HD + spot % LANES
    spread = (real[None] & (column[None] == jnp.arange(inner)[:, None])).astype(low)
    window = -(-inner // LANES) * LANES
    narrow = jnp.stack(
        [
            real[:, None]
            & (column[:, None] + index * (inner % LANES) == jnp.arange(window)[None, :])
            for index in range(3)
        ]
    ).astype(low)
    weight = jnp.einsum("dke,eh->kdh", project_weight, spread, preferred_element_type=low)
    last = jnp.einsum("ed,eh->hd", output_weight, spread, preferred_element_type=low)
    pad = LANES - HD
    gains = jnp.pad(jnp.stack([query_gain, key_gain]).astype(jnp.float32), ((0, 6), (0, pad)))
    return turn_tables(length), gains, narrow, weight, last


def line_sems(count, gathers, sums):
    return [
        pltpu.SemaphoreType.DMA((2,)),
        pltpu.SemaphoreType.DMA((gathers, 2, count)),
        pltpu.SemaphoreType.DMA((gathers, 2, count)),
        pltpu.SemaphoreType.DMA((sums, 2, count, CHUNKS)),
        pltpu.SemaphoreType.DMA((sums, 2, count, CHUNKS)),
    ]


def attend_pass(mod_in, arrays):
    count = lax.axis_size("tensor")
    tables, gains, _, weight, last = arrays
    item = mod_in.shape
    inner = last.shape[0]
    vmem, any_space = pl.BlockSpec(memory_space=pltpu.VMEM), pl.BlockSpec(memory_space=pl.ANY)
    low = jnp.bfloat16
    return pl.pallas_call(
        functools.partial(attend_kernel, count),
        out_shape=(
            jax.ShapeDtypeStruct(item, jnp.float32),
            jax.ShapeDtypeStruct((count, *item), low),
        ),
        in_specs=[vmem, vmem, vmem, any_space, any_space],
        out_specs=(vmem, vmem),
        scratch_shapes=[
            pltpu.VMEM(weight.shape, low),
            pltpu.VMEM(last.shape, low),
            pltpu.VMEM((count, *item), low),
            pltpu.VMEM((3, item[0], inner), jnp.float32),
            pltpu.VMEM((item[0], inner), low),
            pltpu.VMEM((count, *item), low),
            pltpu.VMEM((count + 1, *item), low),
            *line_sems(count, 1, 1),
        ],
        compiler_params=pltpu.CompilerParams(
            collective_id=6, has_side_effects=True, vmem_limit_bytes=60000000
        ),
        name="attend_pass",
    )(mod_in, tables, gains, weight, last)


def attend_back_pass(attend_grad, mod_all, arrays, feed_weights):
    count, wide = lax.axis_size("tensor"), lax.axis_size("dp")
    tables, gains, narrow, weight, last = arrays
    item = attend_grad.shape
    length, width = item
    inner = last.shape[0]
    vmem, any_space = pl.BlockSpec(memory_space=pltpu.VMEM), pl.BlockSpec(memory_space=pl.ANY)
    low, high = jnp.bfloat16, jnp.float32
    window = narrow.shape[2]
    first_width = 3 * window - 2 * LANES
    columns = first_width + window
    if width % (16 * wide):
        wide = 0
    size = width // wide if wide else width
    outs = [
        jax.ShapeDtypeStruct(item, high),
        jax.ShapeDtypeStruct((size, columns), high if wide else low),
        jax.ShapeDtypeStruct((2, 8, LANES), high),
    ]
    scratch = [
        pltpu.VMEM(weight.shape, low),
        pltpu.VMEM(last.shape, low),
        pltpu.VMEM((count, *item), low),
        pltpu.VMEM((3, length, inner), high),
        pltpu.VMEM((length, inner), low),
        pltpu.VMEM((length, inner), low),
        pltpu.VMEM((3, length, inner), low),
        pltpu.VMEM((count, length, first_width), low),
        pltpu.VMEM((count, length, window), low),
        pltpu.VMEM((count, *item), low),
        pltpu.VMEM((count + 1, *item), low),
        pltpu.VMEM((width, columns), high),
        *line_sems(count, 1, 1),
    ]
    ins = [attend_grad, mod_all, tables, gains, narrow, weight, last]
    specs = [vmem, vmem, vmem, vmem, vmem, any_space, any_space]
    if wide:
        ins.append(feed_weights)
        specs.append(any_space)
        kinds, _, units = feed_weights.shape
        outs.append(jax.ShapeDtypeStruct((kinds, size, units), high))
        half = wide // 2
        scratch += [
            pltpu.VMEM((wide, kinds, size, units), low),
            pltpu.VMEM((width, columns), low),
            pltpu.VMEM((half, size, columns), low),
            pltpu.VMEM((half, size, columns), low),
        ]
        for number in (wide, wide, half, half, half, half):
            scratch.append(pltpu.SemaphoreType.DMA((number,)))
    results = pl.pallas_call(
        functools.partial(attend_back_kernel, count, wide),
        out_shape=tuple(outs),
        in_specs=specs,
        out_specs=tuple([vmem] * len(outs)),
        scratch_shapes=scratch,
        compiler_params=pltpu.CompilerParams(
            collective_id=7, has_side_effects=True, vmem_limit_bytes=66000000
        ),
        name="attend_back_pass",
    )(*ins)
    if wide:
        return results

    def scatter(value, axis):
        return lax.psum_scatter(value, "dp", scatter_dimension=axis, tiled=True).astype(high)

    back, weights, gain_parts = results
    return back, scatter(weights, 0), gain_parts, scatter(feed_weights, 1)


def tail_kernel(
    grads_ref,
    small_ref,
    weight_ref,
    slope_ref,
    forward_ref,
    feat_ref,
    label_ref,
    rows_ref,
    pick_ref,
    small_out,
    modulate_out,
    embed_out,
    class_out,
    time_out,
    bias_out,
    grads_land,
    grads_mine,
    grads_land_dp,
    small_one,
    small_mid,
    small_two,
    part,
    part_land,
    cond,
    cond_land,
    forward_land,
    feat_land,
    label_land,
    grads_all,
    cond_all,
    forward_all,
    feat_all,
    label_all,
    *sems,
):
    deep, wide = part_land.shape[0], cond_land.shape[0]
    items = cond.shape[0]
    axes = (("dp", wide), ("tensor", deep))
    hello = pltpu.get_barrier_semaphore()
    for axis, count in axes:
        here = lax.axis_index(axis)

        @pl.loop(1, count)
        def _(offset):
            pl.semaphore_signal(
                hello, inc=1, device_id={axis: lax.rem(here + offset, count)}
            )

    pl.semaphore_wait(hello, wide + deep - 2)
    low = jnp.bfloat16

    def exchange(number, axis, source, target, split=False):
        count = target.shape[0]
        here = lax.axis_index(axis)
        send, recv = sems[2 * number], sems[2 * number + 1]

        def copy(peer, slot):
            return pltpu.make_async_remote_copy(
                src_ref=source.at[peer] if split else source,
                dst_ref=target.at[slot],
                send_sem=send.at[peer],
                recv_sem=recv.at[slot],
                device_id={axis: peer},
            )

        def start():
            @pl.loop(1, count)
            def _(offset):
                copy(lax.rem(here + offset, count), here).start()

            target[here] = source[here] if split else source[...]

        def finish():
            @pl.loop(1, count)
            def _(offset):
                peer = lax.rem(here + offset, count)
                copy(peer, here).wait_send()
                copy(peer, peer).wait_recv()

        return start, finish

    start_grads, finish_grads = exchange(0, "tensor", grads_ref, grads_land, True)
    start_small, finish_small = exchange(1, "dp", small_ref, small_one)
    start_sums, finish_sums = exchange(2, "tensor", small_mid, small_two)
    start_part, finish_part = exchange(3, "tensor", part, part_land)
    start_mine, finish_mine = exchange(4, "dp", grads_mine, grads_land_dp)
    start_cond, finish_cond = exchange(5, "dp", cond, cond_land)
    start_forward, finish_forward = exchange(6, "dp", forward_ref, forward_land, True)
    start_feat, finish_feat = exchange(7, "dp", feat_ref, feat_land)
    start_label, finish_label = exchange(8, "dp", label_ref, label_land)

    start_grads()
    start_small()
    start_forward()
    start_feat()
    start_label()
    finish_grads()
    kinds = grads_mine.shape[0]
    for item in range(items):
        piece = grads_land[item].astype(jnp.float32)
        for kind in range(kinds):
            grads_all[kind, item : item + 1, :] = piece[kind : kind + 1, :]
    total = jnp.zeros(part.shape, jnp.float32)
    for kind in range(kinds):
        mine = grads_all[kind, :items, :].astype(low)
        grads_mine[kind] = mine
        total += dot_rt(mine, weight_ref[kind])
    part[...] = total
    start_part()
    start_mine()
    finish_small()
    small_mid[...] = small_one[0]

    @pl.loop(1, wide)
    def _(index):
        small_mid[...] += small_one[index]

    start_sums()
    finish_part()
    total = part_land[0]
    for index in range(1, deep):
        total += part_land[index]
    cond[...] = (total * slope_ref[...]).astype(low)
    start_cond()
    finish_forward()
    finish_feat()
    finish_label()
    for index in range(wide):
        rows = pl.ds(index * items, items)
        for kind in range(forward_all.shape[0]):
            forward_all[kind, rows, :] = forward_land[index, kind]
        feat_all[rows, :] = feat_land[index]
        label_all[rows, :] = label_land[index]
    finish_mine()
    for index in range(wide):
        rows = pl.ds(index * items, items)
        for kind in range(kinds):
            grads_all[kind, rows, :] = grads_land_dp[index, kind].astype(jnp.float32)
    active = forward_all[0].astype(low)
    for kind in range(kinds):
        modulate_out[kind] = dot_lt(active, grads_all[kind].astype(low))
    finish_sums()
    small_out[...] = small_two[0]

    @pl.loop(1, deep)
    def _(index):
        small_out[...] += small_two[index]

    finish_cond()
    for index in range(wide):
        cond_all[pl.ds(index * items, items), :] = cond_land[index].astype(jnp.float32)
    every = cond_all[...].astype(low)
    embed_out[...] = dot_lt(forward_all[1].astype(low), every)
    picked = dot(every, pick_ref[...]).astype(low)
    classes = class_out.shape[0]
    label = jnp.broadcast_to(label_all[:, 0:1], (label_all.shape[0], classes))
    lane = lax.broadcasted_iota(jnp.int32, label.shape, 1)
    hot = jnp.where(label == lane, 1.0, 0.0).astype(low)
    class_out[...] = dot_lt(hot, picked)
    earlier = (dot_rt(every, rows_ref[...]) * forward_all[2]).astype(low)
    time_out[...] = dot_lt(feat_all[...].astype(low), earlier)
    bias_out[0:1, :] = jnp.sum(picked.astype(jnp.float32), axis=0, keepdims=True)
    bias_out[1:2, :] = jnp.sum(earlier.astype(jnp.float32), axis=0, keepdims=True)


def tail_pass(grads, small, weight, slope, forward, feat, label, rows, pick, classes):
    deep, kinds, slab = grads.shape
    wide, parts, items, share = forward.shape
    width = weight.shape[1]
    batch = wide * items
    freq = feat.shape[1]
    low, high = jnp.bfloat16, jnp.float32
    vmem = pl.BlockSpec(memory_space=pltpu.VMEM)
    shapes = (
        (small.shape, high),
        ((kinds, share, slab), high),
        ((share, width), high),
        ((classes, share), high),
        ((freq, share), high),
        ((2, share), high),
    )
    scratch = (
        ((deep, kinds, slab), low),
        ((kinds, items, slab), low),
        ((wide, kinds, items, slab), low),
        ((wide, *small.shape), high),
        (small.shape, high),
        ((deep, *small.shape), high),
        ((items, width), high),
        ((deep, items, width), high),
        ((items, width), low),
        ((wide, items, width), low),
        (forward.shape, high),
        ((wide, items, freq), high),
        ((wide, items, LANES), jnp.int32),
        ((kinds, batch, slab), high),
        ((batch, width), high),
        ((parts, batch, share), high),
        ((batch, freq), high),
        ((batch, LANES), jnp.int32),
    )
    sems = []
    for number in (deep, wide, deep, deep, wide, wide, wide, wide, wide):
        sems += [pltpu.SemaphoreType.DMA((number,))] * 2
    return pl.pallas_call(
        tail_kernel,
        out_shape=tuple(jax.ShapeDtypeStruct(*shape) for shape in shapes),
        in_specs=[vmem] * 9,
        out_specs=tuple([vmem] * 6),
        scratch_shapes=[pltpu.VMEM(*shape) for shape in scratch] + sems,
        compiler_params=pltpu.CompilerParams(
            collective_id=3, has_side_effects=True, vmem_limit_bytes=60000000
        ),
        name="tail_pass",
    )(grads, small, weight, slope, forward, feat, label, rows, pick)


def shards(
    tokens,
    timesteps,
    labels,
    item_counts,
    cotangent,
    project_weight,
    query_gain,
    key_gain,
    output_weight,
    output_bias,
    expand_weight,
    down_weight,
    down_bias,
    modulate_weight,
    modulate_bias,
    time_weight,
    time_bias,
    embed_weight,
    embed_bias,
    class_table,
):
    local_items, length, width = tokens.shape
    items = timesteps.shape[0]
    slab = modulate_weight.shape[2]
    heads_here = project_weight.shape[2] // HD
    scale = HD ** (-0.5)
    first_item = lax.axis_index("tensor") * local_items
    live = (first_item + jnp.arange(local_items) < item_counts[0]).astype(jnp.float32)[
        :, None, None
    ]
    index = lax.axis_index("dp")
    time_feat = time_features(timesteps).astype(jnp.bfloat16)
    pre_hidden = jnp.dot(
        time_feat, time_weight, preferred_element_type=jnp.float32
    ) + time_bias.astype(jnp.float32)
    time_hidden = jax.nn.silu(pre_hidden).astype(jnp.bfloat16)
    condition = (
        jnp.dot(time_hidden, embed_weight, preferred_element_type=jnp.float32)
        + embed_bias.astype(jnp.float32)
        + jnp.take(class_table, labels, axis=0).astype(jnp.float32)
    )
    cond_act = jax.nn.silu(condition).astype(jnp.bfloat16)
    modulation_part = (
        jnp.einsum("bd,dke->bke", cond_act, modulate_weight, preferred_element_type=jnp.float32)
        + modulate_bias.astype(jnp.float32)
    ).astype(jnp.bfloat16)
    (modulation_local,) = swap("modulation_swap", 2, [(modulation_part, "tensor", True)])
    modulation_local = jnp.transpose(modulation_local, (1, 0, 2)).reshape(1, 6, width)
    modulation_local = modulation_local.astype(jnp.float32)
    local_parts = [modulation_local[:, which][:, None, :] for which in range(6)]
    attend_shift, attend_scale, attend_gate, feed_shift, feed_scale, feed_gate = local_parts
    positions = jnp.arange(length)
    token_local = tokens.astype(jnp.float32)
    normed_local, inverse_local = layer_norm(token_local)
    mod_in = normed_local * (1.0 + attend_scale) + attend_shift
    arrays = attend_arrays(project_weight, output_weight, query_gain, key_gain, length)
    attend_total, mod_all = attend_pass(mod_in[0].astype(jnp.bfloat16), arrays)
    attend_branch = attend_total[None] + output_bias.astype(jnp.float32)
    residual = token_local + attend_gate * attend_branch
    normed_two, inverse_two = layer_norm(residual)
    mod_two = (normed_two * (1.0 + feed_scale) + feed_shift).astype(jnp.bfloat16)
    out_grad = cotangent.astype(jnp.float32) * live
    branch_grad = (out_grad * feed_gate).astype(jnp.bfloat16)
    down_bias_part = jnp.sum(branch_grad.astype(jnp.float32), axis=(0, 1))
    feed_total, mod_two_grad, feed_weights = feed_pass(
        mod_two[0], branch_grad[0], expand_weight, down_weight
    )
    feed_branch = feed_total[None] + down_bias.astype(jnp.float32)
    result = (live * (residual + feed_gate * feed_branch)).astype(jnp.bfloat16)
    mod_two_grad = mod_two_grad[None]
    residual_grad = out_grad + layer_norm_back(
        normed_two, inverse_two, mod_two_grad * (1.0 + feed_scale)
    )
    attend_grad = (residual_grad * attend_gate).astype(jnp.bfloat16)
    output_bias_part = jnp.sum(attend_grad.astype(jnp.float32), axis=(0, 1))
    mod_in_grad, attend_weights, gain_parts, feed_weights = attend_back_pass(
        attend_grad[0], mod_all, arrays, feed_weights
    )
    mod_in_grad = mod_in_grad[None]
    query_gain_part, key_gain_part = jnp.sum(gain_parts, axis=1)[:, :HD]
    tokens_grad = (
        residual_grad
        + layer_norm_back(normed_local, inverse_local, mod_in_grad * (1.0 + attend_scale))
    ).astype(jnp.bfloat16)
    modulation_grad_part = jnp.stack(
        [
            jnp.sum(mod_in_grad, axis=1),
            jnp.sum(mod_in_grad * normed_local, axis=1),
            jnp.sum(residual_grad * attend_branch, axis=1),
            jnp.sum(mod_two_grad, axis=1),
            jnp.sum(mod_two_grad * normed_two, axis=1),
            jnp.sum(out_grad * feed_branch, axis=1),
        ],
        axis=1,
    )
    modulation_grad_part = modulation_grad_part[0].astype(jnp.bfloat16)
    small = jnp.concatenate(
        [
            output_bias_part,
            down_bias_part,
            modulation_grad_part.astype(jnp.float32).reshape(-1),
            query_gain_part,
            key_gain_part,
        ]
    )
    small_size = small.shape[0]
    small = jnp.pad(small, (0, -small_size % 1024)).reshape(-1, 128)
    tensor_size, wide = width // slab, lax.axis_size("dp")
    share = width // wide

    def shares(value):
        return jnp.transpose(value.astype(jnp.float32).reshape(items, wide, share), (1, 0, 2))

    def mine(value):
        return lax.dynamic_slice_in_dim(value, index * share, share, 0)

    pick = jnp.arange(width)[:, None] == index * share + jnp.arange(share)[None, :]
    small, modulate_grad, embed_grad, class_grad, time_grad, biases = tail_pass(
        jnp.transpose(modulation_grad_part.reshape(6, tensor_size, slab), (1, 0, 2)),
        small,
        jnp.transpose(modulate_weight, (1, 0, 2)),
        silu_slope(condition),
        jnp.stack([shares(cond_act), shares(time_hidden), shares(silu_slope(pre_hidden))], axis=1),
        time_feat.astype(jnp.float32),
        jnp.broadcast_to(labels[:, None], (items, LANES)),
        mine(embed_weight),
        pick.astype(jnp.bfloat16),
        class_table.shape[0],
    )
    modulate_grad = jnp.transpose(modulate_grad, (1, 0, 2))
    embed_bias_grad, time_bias_grad = biases
    small = small.reshape(-1)
    output_bias_grad = small[:width]
    down_bias_grad = small[width : 2 * width]
    modulate_bias_grad = small[2 * width : 8 * width].reshape(6, width)
    query_gain_grad = small[8 * width : 8 * width + HD]
    key_gain_grad = small[8 * width + HD : 8 * width + 2 * HD]
    inner = heads_here * HD
    first_width = attend_weights.shape[1] - -(-inner // LANES) * LANES
    project_grad = attend_weights[:, : 3 * inner].reshape(-1, 3, inner)
    output_weight_grad = attend_weights[:, first_width : first_width + inner].T
    expand_grad = jnp.transpose(feed_weights[:2], (1, 0, 2))
    down_grad = feed_weights[2].T
    return (
        result,
        tokens_grad,
        project_grad,
        query_gain_grad,
        key_gain_grad,
        output_weight_grad,
        output_bias_grad,
        expand_grad,
        down_grad,
        down_bias_grad,
        modulate_grad,
        modulate_bias_grad,
        time_grad,
        time_bias_grad,
        embed_grad,
        embed_bias_grad,
        class_grad,
    )


def solution(mesh):
    return jax.shard_map(
        shards,
        mesh=mesh,
        in_specs=(
            P(("dp", "tensor"), None, None),
            P("dp"),
            P("dp"),
            P("dp"),
            P(("dp", "tensor"), None, None),
            P(None, None, "tensor"),
            P(),
            P(),
            P("tensor", None),
            P(),
            P(None, None, "tensor"),
            P("tensor", None),
            P(),
            P(None, None, "tensor"),
            P(None, "tensor"),
            P(),
            P(),
            P(),
            P(),
            P(),
        ),
        out_specs=(
            P(("dp", "tensor"), None, None),
            P(("dp", "tensor"), None, None),
            P("dp", None, "tensor"),
            P(),
            P(),
            P("tensor", "dp"),
            P(),
            P("dp", None, "tensor"),
            P("tensor", "dp"),
            P(),
            P("dp", None, "tensor"),
            P(),
            P(None, "dp"),
            P("dp"),
            P("dp", None),
            P("dp"),
            P(None, "dp"),
        ),
        check_vma=False,
    )
```

profile of v0, /device:TPU:0, one launch (start us, length us, event | category | flops | bytes accessed | tf_op | source)
XLA Modules:
  0.0 383.6 jit_solution(9099934787269768147)
XLA Ops:
  2.2 1.3 fusion.74
  4.2 2.5 gather_fusion
  8.0 2.8 fusion.75
  10.9 3.5 fusion.44
  15.0 8.7 %modulation_swap.1 = bf16[4,6,288]{2,1,0:T(8,128)(2,1)} custom-call(bf16[4,6,288]{2,1,0:T(8,128)(2,1)} %fusion.43.refs_0_), custom_call_target="tpu_custom_call" | custom-call | tf_op jit(solution)/shard_map/modulation_swap/pallas_call | solution.py:551
  25.2 1.1 fusion.29.mod_ref
  27.8 3.9 %convolution_bitcast_fusion.weight_hbm = bf16[3,1152,512]{2,1,0:T(8,128)(2,1)} fusion(bf16[1152,3,288]{0,2,1:T(8,128)(2,1)S(1)} %copy-done.25, s32[512]{0:T(512)S(1)} %fusion.57, pred[512]{0:T(512)(128)(4,1)S(1)} %fusion.62), kind=kOutput, calls=%fused_computation.1 | convolution fusion | flops 1019510784 | bytes 5532160 | tf_op jit(solution)/shard_map/dke,eh->kdh/dot_general | solution.py:952
  31.7 1.9 fusion.31.last_hbm
  34.2 76.3 %attend_pass.1 = (f32[256,1152]{1,0:T(8,128)}, bf16[4,256,1152]{2,1,0:T(8,128)(2,1)}) custom-call(bf16[256,1152]{1,0:T(8,128)(2,1)} %fusion.29.mod_ref, f32[3,256,128]{2,1,0:T(8,128)} %pad_maximum_fusion.tables_ref, f32[8,128]{1,0:T(8,128)} %fusion.59.gains_ref, bf16[3,1152,512]{2,1,0:T(8,128)(2,1)} %convolution_bitcast_fusion.weight_hbm, ...), custom_call_target="tpu_custom_call" | custom-call | tf_op jit(solution)/shard_map/attend_pass/pallas_call | solution.py:976
  110.5 1.6 fusion.79
  113.2 1.3 fusion.28
  114.5 4.2 %copy.71 = bf16[1152,2,768]{2,0,1:T(8,128)(2,1)} copy(bf16[1152,2,768]{2,1,0:T(2,128)(2,1)} %param.30) | data formatting | bytes 7077888 | tf_op args[10]
  118.7 113.4 %feed_pass.1 = (f32[256,1152]{1,0:T(8,128)}, f32[256,1152]{1,0:T(8,128)}, bf16[3,1152,768]{2,1,0:T(8,128)(2,1)}) custom-call(bf16[256,1152]{1,0:T(8,128)(2,1)} %get-tuple-element.128.mod_ref, bf16[256,1152]{1,0:T(8,128)(2,1)} %get-tuple-element.129.grad_ref, bf16[2,1152,768]{2,1,0:T(8,128)(2,1)} %bitcast.106, bf16[768,1152]{1,0:T(8,128)(2,1)} %down_hbm.1), custom_call_target="tpu_custom_call" | custom-call | tf_op jit(solution)/shard_map/feed_pass/pallas_call | solution.py:414
  232.1 1.6 fusion.76
  235.4 2.2 convert_reduce_fusion.1
  237.6 1.0 fusion.40.grad_ref
  239.2 1.2 add_convert_fusion.narrow_ref
  240.4 90.6 %attend_back_pass.1 = (f32[256,1152]{1,0:T(8,128)}, f32[144,1280]{1,0:T(8,128)}, f32[2,8,128]{2,1,0:T(8,128)}, f32[3,144,768]{2,1,0:T(8,128)}) custom-call(bf16[256,1152]{1,0:T(8,128)(2,1)} %fusion.40.grad_ref, bf16[4,256,1152]{2,1,0:T(8,128)(2,1)} %get-tuple-element.35.mod_all, f32[3,256,128]{2,1,0:T(8,128)} %pad_maximum_fusion.tables_ref, ...), custom_call_target="tpu_custom_call" | custom-call | tf_op jit(solution)/shard_map/attend_back_pass/pallas_call | solution.py:1051
  331.1 1.5 fusion.77
  332.6 1.8 fusion.14
  337.5 1.7 constant_dynamic-slice_fusion.rows_ref
  339.3 1.1 fusion.24.pick_ref
  340.9 6.6 %copy.55 = bf16[1152,6,288]{2,0,1:T(8,128)(2,1)} copy(bf16[1152,6,288]{0,2,1:T(8,128)(2,1)} %param.33) | data formatting | bytes 7962624 | tf_op args[13]
  348.1 20.6 %tail_pass.1 = (f32[80,128]{1,0:T(8,128)}, f32[6,144,288]{2,1,0:T(8,128)}, f32[144,1152]{1,0:T(8,128)}, f32[1000,144]{1,0:T(8,128)}, f32[256,144]{1,0:T(8,128)}, /*index=5*/f32[2,144]{1,0:T(2,128)}) custom-call(bf16[4,6,288]{2,1,0:T(8,128)(2,1)} %bitcast.109, f32[80,128]{1,0:T(8,128)} %pad_bitcast_fusion.small_ref, bf16[6,1152,288]{2,1,0:T(8,128)(2,1)} %bitcast.105, ...), custom_call_target="tpu_custom_call" | custom-call | tf_op jit(solution)/shard_map/tail_pass/pallas_call | solution.py:1277
  368.8 2.4 copy.62
  374.9 0.9 copy.59
  375.9 1.6 copy.60
  377.5 1.3 fusion.13
  378.8 0.8 slice_bitcast_fusion.1
  379.6 1.6 slice_bitcast_fusion.2
  381.2 1.1 copy.76
  382.7 0.8 copy.77
  (131 shorter events, 18.9 us)
Async XLA Ops:
  0.7 31.0 %copy-start = (bf16[288,1152]{1,0:T(8,128)(2,1)S(1)}, bf16[288,1152]{1,0:T(8,128)(2,1)}, u32[]{:S(2)}) copy-start(bf16[288,1152]{1,0:T(8,128)(2,1)} %param.28) | copy-start | bytes 1990660
  10.9 3.5 copy-start.18
  10.9 13.8 %copy-start.2 = (bf16[1,256,1152]{2,1,0:T(8,128)(2,1)S(1)}, bf16[1,256,1152]{2,1,0:T(8,128)(2,1)}, u32[]{:S(2)}) copy-start(bf16[1,256,1152]{2,1,0:T(8,128)(2,1)} %param.20) | copy-start | bytes 1769476
  25.2 2.6 copy-start.25
  31.7 1.9 copy-start.22
  31.7 1.9 copy-start.23
  34.2 76.3 %copy-start.19 = (bf16[1152]{0:T(1024)(128)(2,1)S(1)}, bf16[1152]{0:T(1024)(128)(2,1)}, u32[]{:S(2)}) copy-start(bf16[1152]{0:T(1024)(128)(2,1)} %param.29) | copy-start | bytes 6916
  112.1 1.1 copy-start.9
  232.1 1.6 copy-start.5
  233.7 0.7 copy-start.20
  233.7 1.3 copy-start.8
  233.7 1.6 copy-start.12
  237.6 1.6 copy-start.6
  331.1 1.6 copy-start.3
  332.6 2.0 copy-start.17
  340.9 6.6 %copy-start.24 = (s32[4]{0:T(128)S(1)}, s32[4]{0:T(128)}, u32[]{:S(2)}) copy-start(s32[4]{0:T(128)} %param.22) | copy-start | bytes 52
  368.8 2.5 copy-start.15
  368.8 3.2 copy-start.16
  368.8 4.4 %copy-start.21 = (f32[2,144]{1,0:T(2,128)S(1)}, f32[2,144]{1,0:T(2,128)}, u32[]{:S(2)}) copy-start(f32[2,144]{1,0:T(2,128)} %get-tuple-element.44) | copy-start | bytes 3460
  368.8 5.6 %copy-start.13 = (f32[144,1280]{1,0:T(8,128)S(1)}, f32[144,1280]{1,0:T(8,128)}, u32[]{:S(2)}) copy-start(f32[144,1280]{1,0:T(8,128)} %get-tuple-element.38) | copy-start | bytes 2211844
  374.5 1.3 copy-start.10
  375.8 1.7 copy-start.7
  375.9 1.6 copy-start.4
  378.8 2.4 copy-start.11
  381.2 1.5 copy-start.14
  381.2 2.4 copy-start.1
where the time goes:
time: 385 us; the launch traced here: 384 us
  Pallas kernels  310 us (81%)
  local copies, waits for them, and re-layouts  32.9 us (9%)
  other arithmetic  25.8 us (7%)
  matrix products  13.4 us (3%)
    pallas_call x1, Pallas kernels, feed_pass(): pl.pallas_call(functools.partial(feed_kernel, count), out_shape=(jax.Shap...  113 us
    pallas_call x1, Pallas kernels, attend_back_pass(): pl.pallas_call(functools.partial(attend_back_kernel, count, wide), out_sh...  90.6 us
    pallas_call x1, Pallas kernels, attend_pass(): pl.pallas_call(functools.partial(attend_kernel, count), out_shape=(jax.Sh...  76.3 us
    pallas_call x1, Pallas kernels, tail_pass(): pl.pallas_call(tail_kernel, out_shape=tuple((jax.ShapeDtypeStruct(*shape)...  20.6 us
    unnamed x60, local copies, waits for them, and re-layouts  20.2 us
    pallas_call x1, Pallas kernels, swap(): pl.pallas_call(functools.partial(swap_kernel, tuple(plan), int(total is n...  8.72 us

commit v1 on v0

--- a/solution.py
+++ b/solution.py
@@ -607,7 +607,27 @@
 def project(mod, weight, raw):
     @pl.loop(0, weight.shape[0])
     def _(index):
-        raw[index] = dot(mod, weight[index])
+        raw[index] = dot_rt(mod, weight[index])
+
+
+def padded_loads(weight_hbm, last_hbm, weight, last, sem):
+    heads = last.shape[0] // LANES
+    loads = []
+    for head in range(heads):
+        rows, to = pl.ds(head * HD, HD), pl.ds(head * LANES, HD)
+        rest = pl.ds(head * LANES + HD, LANES - HD)
+        for part in range(3):
+            weight[part, rest, :] = jnp.zeros((LANES - HD, weight.shape[2]), weight.dtype)
+            loads.append(
+                pltpu.make_async_copy(
+                    weight_hbm.at[part, rows], weight.at[part, to], sem.at[len(loads)]
+                )
+            )
+        last[rest, :] = jnp.zeros((LANES - HD, last.shape[1]), last.dtype)
+        loads.append(pltpu.make_async_copy(last_hbm.at[rows], last.at[to], sem.at[len(loads)]))
+    for load in loads:
+        load.start()
+    return loads
 
 
 def soft(queries, keys):
@@ -638,12 +658,7 @@
     rs_recv,
 ):
     line = Line(count, [(mod_ref, mod_all)], [(part, land)], (ag_send, ag_recv), (rs_send, rs_recv))
-    loads = (
-        pltpu.make_async_copy(weight_hbm, weight, load_sem.at[0]),
-        pltpu.make_async_copy(last_hbm, last, load_sem.at[1]),
-    )
-    for load in loads:
-        load.start()
+    loads = padded_loads(weight_hbm, last_hbm, weight, last, load_sem)
     line.barrier()
     line.start_own()
     mod_all[line.place] = mod_ref[...]
@@ -707,7 +722,6 @@
     mod_all,
     tables_ref,
     gains_ref,
-    narrow_ref,
     weight_hbm,
     last_hbm,
     *rest,
@@ -719,6 +733,7 @@
     (
         weight,
         last,
+        narrow,
         grad_all,
         raw,
         mixed,
@@ -737,12 +752,7 @@
         *rest,
     ) = rest
     line = Line(count, [(grad_ref, grad_all)], [(part, land)], (ag_send, ag_recv), (rs_send, rs_recv))
-    loads = (
-        pltpu.make_async_copy(weight_hbm, weight, load_sem.at[0]),
-        pltpu.make_async_copy(last_hbm, last, load_sem.at[1]),
-    )
-    for load in loads:
-        load.start()
+    loads = padded_loads(weight_hbm, last_hbm, weight, last, load_sem)
     line.barrier(wide or 1)
     line.start_own()
     width = last.shape[1]
@@ -775,6 +785,14 @@
             feed_copy(peer, here).start()
 
     grad_all[line.place] = grad_ref[...]
+    padded_row = lax.broadcasted_iota(jnp.int32, narrow.shape[1:], 0)
+    lane = padded_row & (LANES - 1)
+    column = (padded_row >> 7) * HD + lane
+    target = lax.broadcasted_iota(jnp.int32, narrow.shape[1:], 1)
+    offset = last.shape[0] // LANES * HD % LANES
+    for part_index in range(3):
+        hit = (lane < HD) & (column + part_index * offset == target)
+        narrow[part_index] = jnp.where(hit, 1.0, 0.0).astype(jnp.bfloat16)
     total[...] = jnp.zeros_like(total)
     gain_out[...] = jnp.zeros_like(gain_out)
     for load in loads:
@@ -830,15 +848,15 @@
         @pl.loop(0, wide_count)
         def _(index):
             cols = span(index, wide_size)
-            sums = dot_rt(raw_grad[0], weight[0, cols, :])
-            sums += dot_rt(raw_grad[1], weight[1, cols, :])
-            sums += dot_rt(raw_grad[2], weight[2, cols, :])
+            sums = dot(raw_grad[0], weight[0, :, cols])
+            sums += dot(raw_grad[1], weight[1, :, cols])
+            sums += dot(raw_grad[2], weight[2, :, cols])
             part[item, :, cols] = sums.astype(jnp.bfloat16)
 
     def keep(item):
-        one = dot(raw_grad[0], narrow_ref[0])
-        two = dot(raw_grad[1], narrow_ref[1])
-        three = dot(raw_grad[2], narrow_ref[2])
+        one = dot(raw_grad[0], narrow[0])
+        two = dot(raw_grad[1], narrow[1])
+        three = dot(raw_grad[2], narrow[2])
         side = one.shape[1] - LANES
         low = jnp.bfloat16
         kept[item, :, :side] = one[:, :side].astype(low)
@@ -846,7 +864,7 @@
         kept[item, :, side + LANES : 2 * side] = two[:, LANES:side].astype(low)
         kept[item, :, 2 * side : 2 * side + LANES] = (two[:, side:] + three[:, :LANES]).astype(low)
         kept[item, :, 2 * side + LANES :] = three[:, LANES:].astype(low)
-        kept_mixed[item] = dot(mixed[...], narrow_ref[0]).astype(low)
+        kept_mixed[item] = dot(mixed[...], narrow[0]).astype(low)
 
     def weigh(item):
         @pl.loop(0, tall_count)
@@ -934,31 +952,14 @@
 
 
 def attend_arrays(project_weight, output_weight, query_gain, key_gain, length):
-    inner = project_weight.shape[2]
-    heads = inner // HD
-    low = jnp.bfloat16
-    spot = jnp.arange(heads * LANES)
-    real = spot % LANES < HD
-    column = spot // LANES * HD + spot % LANES
-    spread = (real[None] & (column[None] == jnp.arange(inner)[:, None])).astype(low)
-    window = -(-inner // LANES) * LANES
-    narrow = jnp.stack(
-        [
-            real[:, None]
-            & (column[:, None] + index * (inner % LANES) == jnp.arange(window)[None, :])
-            for index in range(3)
-        ]
-    ).astype(low)
-    weight = jnp.einsum("dke,eh->kdh", project_weight, spread, preferred_element_type=low)
-    last = jnp.einsum("ed,eh->hd", output_weight, spread, preferred_element_type=low)
-    pad = LANES - HD
-    gains = jnp.pad(jnp.stack([query_gain, key_gain]).astype(jnp.float32), ((0, 6), (0, pad)))
-    return turn_tables(length), gains, narrow, weight, last
-
-
-def line_sems(count, gathers, sums):
+    gains = jnp.stack([query_gain, key_gain]).astype(jnp.float32)
+    gains = jnp.pad(gains, ((0, 6), (0, LANES - HD)))
+    return turn_tables(length), gains, jnp.transpose(project_weight, (1, 2, 0)), output_weight
+
+
+def line_sems(count, gathers, sums, loads=2):
     return [
-        pltpu.SemaphoreType.DMA((2,)),
+        pltpu.SemaphoreType.DMA((loads,)),
         pltpu.SemaphoreType.DMA((gathers, 2, count)),
         pltpu.SemaphoreType.DMA((gathers, 2, count)),
         pltpu.SemaphoreType.DMA((sums, 2, count, CHUNKS)),
@@ -968,9 +969,11 @@
 
 def attend_pass(mod_in, arrays):
     count = lax.axis_size("tensor")
-    tables, gains, _, weight, last = arrays
+    tables, gains, weight, last = arrays
     item = mod_in.shape
-    inner = last.shape[0]
+    width = item[1]
+    heads = last.shape[0] // HD
+    inner = heads * LANES
     vmem, any_space = pl.BlockSpec(memory_space=pltpu.VMEM), pl.BlockSpec(memory_space=pl.ANY)
     low = jnp.bfloat16
     return pl.pallas_call(
@@ -982,14 +985,14 @@
         in_specs=[vmem, vmem, vmem, any_space, any_space],
         out_specs=(vmem, vmem),
         scratch_shapes=[
-            pltpu.VMEM(weight.shape, low),
-            pltpu.VMEM(last.shape, low),
+            pltpu.VMEM((3, inner, width), low),
+            pltpu.VMEM((inner, width), low),
             pltpu.VMEM((count, *item), low),
             pltpu.VMEM((3, item[0], inner), jnp.float32),
             pltpu.VMEM((item[0], inner), low),
             pltpu.VMEM((count, *item), low),
             pltpu.VMEM((count + 1, *item), low),
-            *line_sems(count, 1, 1),
+            *line_sems(count, 1, 1, 4 * heads),
         ],
         compiler_params=pltpu.CompilerParams(
             collective_id=6, has_side_effects=True, vmem_limit_bytes=60000000
@@ -1000,13 +1003,14 @@
 
 def attend_back_pass(attend_grad, mod_all, arrays, feed_weights):
     count, wide = lax.axis_size("tensor"), lax.axis_size("dp")
-    tables, gains, narrow, weight, last = arrays
+    tables, gains, weight, last = arrays
     item = attend_grad.shape
     length, width = item
-    inner = last.shape[0]
+    heads = last.shape[0] // HD
+    inner = heads * LANES
     vmem, any_space = pl.BlockSpec(memory_space=pltpu.VMEM), pl.BlockSpec(memory_space=pl.ANY)
     low, high = jnp.bfloat16, jnp.float32
-    window = narrow.shape[2]
+    window = -(-last.shape[0] // LANES) * LANES
     first_width = 3 * window - 2 * LANES
     columns = first_width + window
     if width % (16 * wide):
@@ -1018,8 +1022,9 @@
         jax.ShapeDtypeStruct((2, 8, LANES), high),
     ]
     scratch = [
-        pltpu.VMEM(weight.shape, low),
-        pltpu.VMEM(last.shape, low),
+        pltpu.VMEM((3, inner, width), low),
+        pltpu.VMEM((inner, width), low),
+        pltpu.VMEM((3, inner, window), low),
         pltpu.VMEM((count, *item), low),
         pltpu.VMEM((3, length, inner), high),
         pltpu.VMEM((length, inner), low),
@@ -1030,10 +1035,10 @@
         pltpu.VMEM((count, *item), low),
         pltpu.VMEM((count + 1, *item), low),
         pltpu.VMEM((width, columns), high),
-        *line_sems(count, 1, 1),
+        *line_sems(count, 1, 1, 4 * heads),
     ]
-    ins = [attend_grad, mod_all, tables, gains, narrow, weight, last]
-    specs = [vmem, vmem, vmem, vmem, vmem, any_space, any_space]
+    ins = [attend_grad, mod_all, tables, gains, weight, last]
+    specs = [vmem, vmem, vmem, vmem, any_space, any_space]
     if wide:
         ins.append(feed_weights)
         specs.append(any_space)
@@ -1077,8 +1082,7 @@
     forward_ref,
     feat_ref,
     label_ref,
-    rows_ref,
-    pick_ref,
+    rows_hbm,
     small_out,
     modulate_out,
     embed_out,
@@ -1103,10 +1107,19 @@
     forward_all,
     feat_all,
     label_all,
+    rows,
+    load_sem,
     *sems,
 ):
     deep, wide = part_land.shape[0], cond_land.shape[0]
     items = cond.shape[0]
+    share = rows.shape[0]
+    seat = lax.axis_index("dp") * share
+    start_row = seat if rows_hbm.shape[0] > share else 0
+    if share % 16 == 0:
+        start_row = pl.multiple_of(start_row, 16)
+    load = pltpu.make_async_copy(rows_hbm.at[pl.ds(start_row, share)], rows, load_sem)
+    load.start()
     axes = (("dp", wide), ("tensor", deep))
     hello = pltpu.get_barrier_semaphore()
     for axis, count in axes:
@@ -1176,7 +1189,7 @@
     for kind in range(kinds):
         mine = grads_all[kind, :items, :].astype(low)
         grads_mine[kind] = mine
-        total += dot_rt(mine, weight_ref[kind])
+        total += dot(mine, weight_ref[kind])
     part[...] = total
     start_part()
     start_mine()
@@ -1198,16 +1211,16 @@
     finish_feat()
     finish_label()
     for index in range(wide):
-        rows = pl.ds(index * items, items)
+        batch = pl.ds(index * items, items)
         for kind in range(forward_all.shape[0]):
-            forward_all[kind, rows, :] = forward_land[index, kind]
-        feat_all[rows, :] = feat_land[index]
-        label_all[rows, :] = label_land[index]
+            forward_all[kind, batch, :] = forward_land[index, kind]
+        feat_all[batch, :] = feat_land[index]
+        label_all[batch, :] = label_land[index]
     finish_mine()
     for index in range(wide):
-        rows = pl.ds(index * items, items)
+        batch = pl.ds(index * items, items)
         for kind in range(kinds):
-            grads_all[kind, rows, :] = grads_land_dp[index, kind].astype(jnp.float32)
+            grads_all[kind, batch, :] = grads_land_dp[index, kind].astype(jnp.float32)
     active = forward_all[0].astype(low)
     for kind in range(kinds):
         modulate_out[kind] = dot_lt(active, grads_all[kind].astype(low))
@@ -1223,22 +1236,26 @@
         cond_all[pl.ds(index * items, items), :] = cond_land[index].astype(jnp.float32)
     every = cond_all[...].astype(low)
     embed_out[...] = dot_lt(forward_all[1].astype(low), every)
-    picked = dot(every, pick_ref[...]).astype(low)
-    classes = class_out.shape[0]
+    width = every.shape[1]
+    spot = lax.broadcasted_iota(jnp.int32, (width, share), 0)
+    pick = jnp.where(spot == seat + lax.broadcasted_iota(jnp.int32, (width, share), 1), 1.0, 0.0)
+    picked = dot(every, pick.astype(low)).astype(low)
+    classes = class_out.shape[1]
     label = jnp.broadcast_to(label_all[:, 0:1], (label_all.shape[0], classes))
     lane = lax.broadcasted_iota(jnp.int32, label.shape, 1)
     hot = jnp.where(label == lane, 1.0, 0.0).astype(low)
-    class_out[...] = dot_lt(hot, picked)
-    earlier = (dot_rt(every, rows_ref[...]) * forward_all[2]).astype(low)
-    time_out[...] = dot_lt(feat_all[...].astype(low), earlier)
+    class_out[...] = dot_lt(picked, hot)
+    load.wait()
+    earlier = (dot_rt(every, rows[...]) * forward_all[2]).astype(low)
+    time_out[...] = dot_lt(earlier, feat_all[...].astype(low))
     bias_out[0:1, :] = jnp.sum(picked.astype(jnp.float32), axis=0, keepdims=True)
     bias_out[1:2, :] = jnp.sum(earlier.astype(jnp.float32), axis=0, keepdims=True)
 
 
-def tail_pass(grads, small, weight, slope, forward, feat, label, rows, pick, classes):
+def tail_pass(grads, small, weight, slope, forward, feat, label, rows, classes):
     deep, kinds, slab = grads.shape
     wide, parts, items, share = forward.shape
-    width = weight.shape[1]
+    width = weight.shape[2]
     batch = wide * items
     freq = feat.shape[1]
     low, high = jnp.bfloat16, jnp.float32
@@ -1247,8 +1264,8 @@
         (small.shape, high),
         ((kinds, share, slab), high),
         ((share, width), high),
-        ((classes, share), high),
-        ((freq, share), high),
+        ((share, classes), high),
+        ((share, freq), high),
         ((2, share), high),
     )
     scratch = (
@@ -1270,21 +1287,22 @@
         ((parts, batch, share), high),
         ((batch, freq), high),
         ((batch, LANES), jnp.int32),
-    )
-    sems = []
+        ((share, width), low),
+    )
+    sems = [pltpu.SemaphoreType.DMA]
     for number in (deep, wide, deep, deep, wide, wide, wide, wide, wide):
         sems += [pltpu.SemaphoreType.DMA((number,))] * 2
     return pl.pallas_call(
         tail_kernel,
         out_shape=tuple(jax.ShapeDtypeStruct(*shape) for shape in shapes),
-        in_specs=[vmem] * 9,
+        in_specs=[vmem] * 7 + [pl.BlockSpec(memory_space=pl.ANY)],
         out_specs=tuple([vmem] * 6),
         scratch_shapes=[pltpu.VMEM(*shape) for shape in scratch] + sems,
         compiler_params=pltpu.CompilerParams(
             collective_id=3, has_side_effects=True, vmem_limit_bytes=60000000
         ),
         name="tail_pass",
-    )(grads, small, weight, slope, forward, feat, label, rows, pick)
+    )(grads, small, weight, slope, forward, feat, label, rows)
 
 
 def shards(
@@ -1327,7 +1345,7 @@
     condition = (
         jnp.dot(time_hidden, embed_weight, preferred_element_type=jnp.float32)
         + embed_bias.astype(jnp.float32)
-        + jnp.take(class_table, labels, axis=0).astype(jnp.float32)
+        + class_table.at[labels].get(mode="promise_in_bounds").astype(jnp.float32)
     )
     cond_act = jax.nn.silu(condition).astype(jnp.bfloat16)
     modulation_part = (
@@ -1401,22 +1419,21 @@
     def shares(value):
         return jnp.transpose(value.astype(jnp.float32).reshape(items, wide, share), (1, 0, 2))
 
-    def mine(value):
-        return lax.dynamic_slice_in_dim(value, index * share, share, 0)
-
-    pick = jnp.arange(width)[:, None] == index * share + jnp.arange(share)[None, :]
+    rows = embed_weight
+    if share % 16:
+        rows = lax.dynamic_slice_in_dim(embed_weight, index * share, share, 0)
     small, modulate_grad, embed_grad, class_grad, time_grad, biases = tail_pass(
         jnp.transpose(modulation_grad_part.reshape(6, tensor_size, slab), (1, 0, 2)),
         small,
-        jnp.transpose(modulate_weight, (1, 0, 2)),
+        jnp.transpose(modulate_weight, (1, 2, 0)),
         silu_slope(condition),
         jnp.stack([shares(cond_act), shares(time_hidden), shares(silu_slope(pre_hidden))], axis=1),
         time_feat.astype(jnp.float32),
         jnp.broadcast_to(labels[:, None], (items, LANES)),
-        mine(embed_weight),
-        pick.astype(jnp.bfloat16),
+        rows,
         class_table.shape[0],
     )
+    class_grad, time_grad = class_grad.T, time_grad.T
     modulate_grad = jnp.transpose(modulate_grad, (1, 0, 2))
     embed_bias_grad, time_bias_grad = biases
     small = small.reshape(-1)

time: 385 us -> 367 us (0.953)
  matrix products: 13.4 us -> 6.56 us
  local copies, waits for them, and re-layouts: 32.9 us -> 26.3 us
    unnamed x60 -> x53, local copies, waits for them, and re-layouts: 20.2 us -> 13.2 us
    dot_general x2 -> x0, matrix products: 5.82 us -> none  [the longest x1 3.92 us: attend_arrays(): jnp.einsum('dke,eh->kdh', project_weight, spread, preferred_element_type=...]
where the time goes in v1:
time: 367 us; the launch traced here: 366 us
  Pallas kernels  309 us (84%)
  local copies, waits for them, and re-layouts  26.3 us (7%)
  other arithmetic  22 us (6%)
  matrix products  6.56 us (2%)
    pallas_call x1, Pallas kernels, feed_pass(): pl.pallas_call(functools.partial(feed_kernel, count), out_shape=(jax.Shap...  113 us
    pallas_call x1, Pallas kernels, attend_back_pass(): pl.pallas_call(functools.partial(attend_back_kernel, count, wide), out_sh...  91.2 us
    pallas_call x1, Pallas kernels, attend_pass(): pl.pallas_call(functools.partial(attend_kernel, count), out_shape=(jax.Sh...  76.9 us
    pallas_call x1, Pallas kernels, tail_pass(): pl.pallas_call(tail_kernel, out_shape=tuple((jax.ShapeDtypeStruct(*shape)...  18.9 us
    unnamed x53, local copies, waits for them, and re-layouts  13.2 us
    pallas_call x1, Pallas kernels, swap(): pl.pallas_call(functools.partial(swap_kernel, tuple(plan), int(total is n...  8.72 us

profile of v1, /device:TPU:0, one launch (start us, length us, event | category | flops | bytes accessed | tf_op | source)
XLA Modules:
  0.0 365.7 jit_solution(1005009940636998642)
XLA Ops:
  0.7 0.7 convert_element_type.136
  3.1 2.5 gather_fusion
  6.3 2.8 fusion.54
  9.2 3.5 fusion.31
  13.3 8.7 %modulation_swap.1 = bf16[4,6,288]{2,1,0:T(8,128)(2,1)} custom-call(bf16[4,6,288]{2,1,0:T(8,128)(2,1)} %fusion.30.refs_0_), custom_call_target="tpu_custom_call" | custom-call | tf_op jit(solution)/shard_map/modulation_swap/pallas_call | solution.py:551
  22.0 0.7 convert_bitcast_fusion
  23.5 1.1 fusion.25.mod_ref
  25.3 0.8 pad_maximum_fusion.tables_ref
  26.6 76.9 %attend_pass.1 = (f32[256,1152]{1,0:T(8,128)}, bf16[4,256,1152]{2,1,0:T(8,128)(2,1)}) custom-call(bf16[256,1152]{1,0:T(8,128)(2,1)} %fusion.25.mod_ref, f32[3,256,128]{2,1,0:T(8,128)} %pad_maximum_fusion.tables_ref, f32[8,128]{1,0:T(8,128)} %fusion.43.gains_ref, bf16[3,288,1152]{2,1,0:T(8,128)(2,1)} %bitcast.103, bf16[288,1152]{1,0:T(8,128)(2,1)} %last_hbm.3), custom_call_target="tpu_custom_call" | custom-call | tf_op jit(solution)/shard_map/attend_pass/pallas_call | solution.py:979
  103.5 1.6 fusion.58
  106.2 1.3 fusion.24
  107.4 4.3 %copy.62 = bf16[1152,2,768]{2,0,1:T(8,128)(2,1)} copy(bf16[1152,2,768]{2,1,0:T(2,128)(2,1)} %param.30) | data formatting | bytes 7077888 | tf_op args[10]
  111.7 113.5 %feed_pass.1 = (f32[256,1152]{1,0:T(8,128)}, f32[256,1152]{1,0:T(8,128)}, bf16[3,1152,768]{2,1,0:T(8,128)(2,1)}) custom-call(bf16[256,1152]{1,0:T(8,128)(2,1)} %get-tuple-element.125.mod_ref, bf16[256,1152]{1,0:T(8,128)(2,1)} %get-tuple-element.126.grad_ref, bf16[2,1152,768]{2,1,0:T(8,128)(2,1)} %bitcast.102, bf16[768,1152]{1,0:T(8,128)(2,1)} %down_hbm.1), custom_call_target="tpu_custom_call" | custom-call | tf_op jit(solution)/shard_map/feed_pass/pallas_call | solution.py:414
  225.2 1.6 fusion.55
  228.5 2.2 convert_reduce_fusion.1
  230.6 1.0 copy-done.5
  231.7 0.9 fusion.27.grad_ref
  232.5 91.2 %attend_back_pass.1 = (f32[256,1152]{1,0:T(8,128)}, f32[144,1280]{1,0:T(8,128)}, f32[2,8,128]{2,1,0:T(8,128)}, f32[3,144,768]{2,1,0:T(8,128)}) custom-call(bf16[256,1152]{1,0:T(8,128)(2,1)} %fusion.27.grad_ref, bf16[4,256,1152]{2,1,0:T(8,128)(2,1)} %get-tuple-element.35.mod_all, f32[3,256,128]{2,1,0:T(8,128)} %pad_maximum_fusion.tables_ref, ...), custom_call_target="tpu_custom_call" | custom-call | tf_op jit(solution)/shard_map/attend_back_pass/pallas_call | solution.py:1056
  323.8 1.5 fusion.56
  325.4 1.8 fusion.14
  331.5 18.9 %tail_pass.1 = (f32[80,128]{1,0:T(8,128)}, f32[6,144,288]{2,1,0:T(8,128)}, f32[144,1152]{1,0:T(8,128)}, f32[144,1000]{1,0:T(8,128)}, f32[144,256]{1,0:T(8,128)}, /*index=5*/f32[2,144]{1,0:T(2,128)}) custom-call(bf16[4,6,288]{2,1,0:T(8,128)(2,1)} %bitcast.109, f32[80,128]{1,0:T(8,128)} %pad_bitcast_fusion.small_ref, bf16[6,288,1152]{2,1,0:T(8,128)(2,1)} %bitcast.101, ...), custom_call_target="tpu_custom_call" | custom-call | tf_op jit(solution)/shard_map/tail_pass/pallas_call | solution.py:1295
  350.4 0.8 slice.71
  351.8 1.4 slice_bitcast_fusion.3
  353.2 1.3 fusion.60
  354.5 1.3 fusion.59
  356.3 0.9 copy.53
  357.9 1.6 copy.54
  359.5 1.3 fusion.13
  360.8 0.8 slice_bitcast_fusion.1
  362.3 1.1 copy.69
  364.1 0.8 copy.71
  364.9 0.8 copy.72
  (113 shorter events, 14.5 us)
Async XLA Ops:
  0.7 1.6 copy-start
  9.2 3.5 copy-start.17
  9.2 13.8 %copy-start.1 = (bf16[1,256,1152]{2,1,0:T(8,128)(2,1)S(1)}, bf16[1,256,1152]{2,1,0:T(8,128)(2,1)}, u32[]{:S(2)}) copy-start(bf16[1,256,1152]{2,1,0:T(8,128)(2,1)} %param.20) | copy-start | bytes 1769476
  23.5 2.6 copy-start.20
  23.5 2.6 copy-start.21
  26.6 76.9 %copy-start.18 = (bf16[1152]{0:T(1024)(128)(2,1)S(1)}, bf16[1152]{0:T(1024)(128)(2,1)}, u32[]{:S(2)}) copy-start(bf16[1152]{0:T(1024)(128)(2,1)} %param.29) | copy-start | bytes 6916
  105.1 1.1 copy-start.8
  225.2 1.6 copy-start.4
  226.8 0.7 copy-start.19
  226.8 1.3 copy-start.7
  226.8 1.6 copy-start.11
  230.6 1.0 copy-start.5
  323.8 1.6 copy-start.2
  325.4 2.0 copy-start.16
  325.4 5.5 %copy-start.22 = (s32[4]{0:T(128)S(1)}, s32[4]{0:T(128)}, u32[]{:S(2)}) copy-start(s32[4]{0:T(128)} %param.22) | copy-start | bytes 52
  331.5 24.3 %copy-start.12 = (f32[144,1280]{1,0:T(8,128)S(1)}, f32[144,1280]{1,0:T(8,128)}, u32[]{:S(2)}) copy-start(f32[144,1280]{1,0:T(8,128)} %get-tuple-element.38) | copy-start | bytes 2211844
  356.3 1.6 copy-start.9
  357.9 1.7 copy-start.6
  357.9 1.6 copy-start.3
  360.8 1.5 copy-start.10
  362.3 1.1 copy-start.15
  362.3 1.7 copy-start.13
  363.4 1.5 copy-start.14

commit v2 on v1

--- a/solution.py
+++ b/solution.py
@@ -35,28 +35,6 @@
     return sigma * (1.0 + value * (1.0 - sigma))
 
 
-def rotate(value, positions):
-    quarter = HD // 4
-    rates = 10000.0 ** (-jnp.arange(quarter, dtype=jnp.float32) / quarter)
-    places = ((positions // GRID).astype(jnp.float32), (positions % GRID).astype(jnp.float32))
-    pieces = []
-    for which_half in range(2):
-        half_value = value[..., which_half * 2 * quarter : (which_half + 1) * 2 * quarter]
-        angle = places[which_half][:, None] * rates[None, :]
-        cosine = jnp.cos(angle)[None, :, None, :]
-        sine = jnp.sin(angle)[None, :, None, :]
-        first = half_value[..., :quarter]
-        second = half_value[..., quarter:]
-        pieces.append(first * cosine - second * sine)
-        pieces.append(second * cosine + first * sine)
-    return jnp.concatenate(pieces, axis=-1)
-
-
-def head_prepare(raw, gain, positions):
-    scaled = raw * lax.rsqrt(jnp.mean(raw * raw, axis=-1, keepdims=True) + EPS) * gain
-    return rotate(scaled, positions)
-
-
 def time_features(steps_in):
     half = FREQ // 2
     rates = jnp.exp(-math.log(10000.0) * jnp.arange(half, dtype=jnp.float32) / half)
@@ -64,17 +42,18 @@
     return jnp.concatenate([jnp.cos(angle), jnp.sin(angle)], axis=-1)
 
 
-CHUNKS = 8
-
-
-def rows_of(block, total):
-    size = total // CHUNKS
+FEED_BLOCKS, ATTEND_BLOCKS = 8, 4
+
+
+def rows_of(block, total, blocks):
+    size = total // blocks
     return pl.ds(pl.multiple_of(block * size, size), size)
 
 
 class Line:
-    def __init__(self, count, gathered, summed, ag_sems, rs_sems):
+    def __init__(self, count, blocks, gathered, summed, ag_sems, rs_sems):
         self.count = count
+        self.blocks = blocks
         self.place = lax.axis_index("tensor")
         self.gathered = gathered
         self.summed = summed
@@ -123,7 +102,7 @@
         slot = item
         if way == 1:
             slot = jnp.where(item == target, self.count, item)
-        rows = rows_of(block, part.shape[1])
+        rows = rows_of(block, part.shape[1], self.blocks)
         return pltpu.make_async_remote_copy(
             src_ref=part.at[item, rows],
             dst_ref=landed.at[slot, rows],
@@ -137,7 +116,7 @@
 
     def wait_sum(self, which, way, item, block):
         part, landed = self.summed[which]
-        rows = rows_of(block, part.shape[1])
+        rows = rows_of(block, part.shape[1], self.blocks)
         view = landed.at[self.landed_slot(way, item), rows]
         pltpu.make_async_remote_copy(
             src_ref=view,
@@ -183,7 +162,7 @@
         )
 
     def first_sums(self, step, arrays=(0,)):
-        @pl.loop(0, CHUNKS)
+        @pl.loop(0, self.blocks)
         def _(block):
             for way, item, further, hop in self.moves(step):
 
@@ -193,17 +172,17 @@
                         self.sum_copy(which, way, item, block).start()
 
     def relay_sums(self, step, arrays=(0,)):
-        @pl.loop(0, CHUNKS + self.count - 3)
+        @pl.loop(0, self.blocks + self.count - 3)
         def _(turn):
             for distance in range(1, self.count - 1):
                 block = turn - (distance - 1)
                 for way, item, further, hop in self.moves(step):
 
-                    @pl.when(further & (hop == distance) & (block >= 0) & (block < CHUNKS))
+                    @pl.when(further & (hop == distance) & (block >= 0) & (block < self.blocks))
                     def _():
                         for which in arrays:
                             part, landed = self.summed[which]
-                            rows = rows_of(block, part.shape[1])
+                            rows = rows_of(block, part.shape[1], self.blocks)
                             view = self.wait_sum(which, way, item, block)
                             total = part[item, rows].astype(jnp.float32) + view[...].astype(
                                 jnp.float32
@@ -234,9 +213,9 @@
         place, count = self.place, self.count
         part, landed = self.summed[which]
 
-        @pl.loop(0, CHUNKS)
+        @pl.loop(0, self.blocks)
         def _(block):
-            rows = rows_of(block, part.shape[1])
+            rows = rows_of(block, part.shape[1], self.blocks)
             out[rows] = part[place, rows].astype(jnp.float32)
             for way in range(2):
 
@@ -262,7 +241,7 @@
 
                 @pl.when(further)
                 def _():
-                    @pl.loop(0, CHUNKS)
+                    @pl.loop(0, self.blocks)
                     def _(block):
                         for which in range(len(self.summed)):
                             self.sum_copy(which, way, item, block).wait_send()
@@ -322,6 +301,7 @@
 ):
     line = Line(
         count,
+        FEED_BLOCKS,
         [(mod_ref, mod_all), (grad_ref, grad_all)],
         [(back_part, back_land), (feed_part, feed_land)],
         (ag_send, ag_recv),
@@ -433,130 +413,13 @@
             pltpu.VMEM((count + 1, *item), low),
             pltpu.VMEM((3, width, units), jnp.float32),
             pltpu.VMEM((3, width, units), low),
-            *line_sems(count, 2, 2),
+            *line_sems(count, FEED_BLOCKS, 2, 2),
         ],
         compiler_params=pltpu.CompilerParams(
             collective_id=1, has_side_effects=True, vmem_limit_bytes=64000000
         ),
         name="feed_pass",
     )(mod_two, branch_grad, expand, down_weight)
-
-
-def swap_kernel(jobs, total, *refs):
-    n = len(jobs)
-    ins, outs = refs[:n], refs[n + total : 2 * n + total]
-    sems = refs[2 * n + 2 * total :]
-    places = [lax.axis_index(axis) for axis, _, _ in jobs]
-    hello = pltpu.get_barrier_semaphore()
-    axes = []
-    for axis, count, _ in jobs:
-        if (axis, count) not in axes:
-            axes.append((axis, count))
-    if total:
-        axes = [("dp", lax.axis_size("dp")), ("tensor", lax.axis_size("tensor"))]
-    for axis, count in axes:
-        here = lax.axis_index(axis)
-
-        @pl.loop(1, count)
-        def _(offset):
-            peer = lax.rem(here + offset, count)
-            pl.semaphore_signal(hello, inc=1, device_id={axis: peer})
-
-    pl.semaphore_wait(hello, sum(count - 1 for _, count in axes))
-
-    def copy(source, target, send, recv, axis, peer, slot):
-        return pltpu.make_async_remote_copy(
-            src_ref=source,
-            dst_ref=target.at[slot],
-            send_sem=send.at[peer],
-            recv_sem=recv.at[slot],
-            device_id={axis: peer},
-        )
-
-    def start(source, target, send, recv, axis, count, split):
-        here = lax.axis_index(axis)
-
-        @pl.loop(1, count)
-        def _(offset):
-            peer = lax.rem(here + offset, count)
-            piece = source.at[peer] if split else source
-            copy(piece, target, send, recv, axis, peer, here).start()
-
-        target[here] = source[here] if split else source[...]
-
-    def finish(source, target, send, recv, axis, count, split):
-        here = lax.axis_index(axis)
-
-        @pl.loop(1, count)
-        def _(offset):
-            peer = lax.rem(here + offset, count)
-            piece = source.at[peer] if split else source
-            step = copy(piece, target, send, recv, axis, peer, peer)
-            step.wait_recv()
-            step.wait_send()
-
-    work = []
-    for index, (axis, count, split) in enumerate(jobs):
-        work.append((ins[index], outs[index], sems[2 * index], sems[2 * index + 1], axis, count, split))
-    if total:
-        source, result = refs[n], refs[2 * n + total]
-        one, two, middle, s1, r1, s2, r2 = sems[2 * n :]
-        wide, deep = lax.axis_size("dp"), lax.axis_size("tensor")
-        first = (source, one, s1, r1, "dp", wide, False)
-        start(*first)
-    for job in work:
-        start(*job)
-    if total:
-        finish(*first)
-        middle[...] = one[0]
-
-        @pl.loop(1, wide)
-        def _(index):
-            middle[...] += one[index]
-
-        second = (middle, two, s2, r2, "tensor", deep, False)
-        start(*second)
-    for job in work:
-        finish(*job)
-    if total:
-        finish(*second)
-        result[...] = two[0]
-
-        @pl.loop(1, deep)
-        def _(index):
-            result[...] += two[index]
-
-
-def swap(name, number, jobs, total=None):
-    vmem = pl.BlockSpec(memory_space=pltpu.VMEM)
-    plan, arrays, shapes, scratch = [], [], [], []
-    for array, axis, split in jobs:
-        count = lax.axis_size(axis)
-        plan.append((axis, count, split))
-        arrays.append(array)
-        piece = array.shape[1:] if split else array.shape
-        shapes.append(jax.ShapeDtypeStruct((count, *piece), array.dtype))
-        scratch += [pltpu.SemaphoreType.DMA((count,)), pltpu.SemaphoreType.DMA((count,))]
-    if total is not None:
-        wide, deep = lax.axis_size("dp"), lax.axis_size("tensor")
-        arrays.append(total)
-        shapes.append(jax.ShapeDtypeStruct(total.shape, total.dtype))
-        scratch += [
-            pltpu.VMEM((wide, *total.shape), total.dtype),
-            pltpu.VMEM((deep, *total.shape), total.dtype),
-            pltpu.VMEM(total.shape, total.dtype),
-        ]
-        for count in (wide, wide, deep, deep):
-            scratch.append(pltpu.SemaphoreType.DMA((count,)))
-    return pl.pallas_call(
-        functools.partial(swap_kernel, tuple(plan), int(total is not None)),
-        out_shape=tuple(shapes),
-        in_specs=[vmem] * len(arrays),
-        out_specs=tuple([vmem] * len(shapes)),
-        scratch_shapes=scratch,
-        compiler_params=pltpu.CompilerParams(collective_id=number, has_side_effects=True),
-        name=name,
-    )(*arrays)
 
 
 LANES = 128
@@ -637,13 +500,17 @@
 
 def attend_kernel(
     count,
-    mod_ref,
+    token_ref,
+    slab_ref,
     tables_ref,
     gains_ref,
     weight_hbm,
     last_hbm,
     branch_out,
     mod_out,
+    rows_out,
+    slab_land,
+    mod_own,
     weight,
     last,
     mod_all,
@@ -656,12 +523,56 @@
     ag_recv,
     rs_send,
     rs_recv,
+    slab_send,
+    slab_recv,
 ):
-    line = Line(count, [(mod_ref, mod_all)], [(part, land)], (ag_send, ag_recv), (rs_send, rs_recv))
+    line = Line(count, ATTEND_BLOCKS, [(mod_own, mod_all)], [(part, land)], (ag_send, ag_recv), (rs_send, rs_recv))
     loads = padded_loads(weight_hbm, last_hbm, weight, last, load_sem)
-    line.barrier()
+    place = line.place
+    hello = pltpu.get_barrier_semaphore()
+
+    @pl.loop(1, count)
+    def _(offset):
+        pl.semaphore_signal(hello, inc=1, device_id={"tensor": lax.rem(place + offset, count)})
+
+    pl.semaphore_wait(hello, count - 1)
+
+    def slab_copy(peer, slot):
+        return pltpu.make_async_remote_copy(
+            src_ref=slab_ref.at[peer],
+            dst_ref=slab_land.at[slot],
+            send_sem=slab_send.at[peer],
+            recv_sem=slab_recv.at[slot],
+            device_id={"tensor": peer},
+        )
+
+    @pl.loop(1, count)
+    def _(offset):
+        slab_copy(lax.rem(place + offset, count), place).start()
+
+    slab_land[place] = slab_ref[place]
+
+    @pl.loop(1, count)
+    def _(offset):
+        peer = lax.rem(place + offset, count)
+        slab_copy(peer, place).wait_send()
+        slab_copy(peer, peer).wait_recv()
+
+    rows_out[...] = jnp.concatenate(
+        [slab_land[index].astype(jnp.float32) for index in range(count)], axis=1
+    )
+
+    @pl.loop(0, ATTEND_BLOCKS)
+    def _(block):
+        rows = rows_of(block, token_ref.shape[0], ATTEND_BLOCKS)
+        value = token_ref[rows].astype(jnp.float32)
+        center = value - jnp.mean(value, axis=-1, keepdims=True)
+        inverse = lax.rsqrt(jnp.mean(center * center, axis=-1, keepdims=True) + EPS)
+        mod = center * inverse * (1.0 + rows_out[1:2, :]) + rows_out[0:1, :]
+        mod_own[rows] = mod.astype(jnp.bfloat16)
+        mod_all[place, rows] = mod.astype(jnp.bfloat16)
+
     line.start_own()
-    mod_all[line.place] = mod_ref[...]
     for load in loads:
         load.wait()
     heads = last.shape[0] // LANES
@@ -751,7 +662,7 @@
         rs_recv,
         *rest,
     ) = rest
-    line = Line(count, [(grad_ref, grad_all)], [(part, land)], (ag_send, ag_recv), (rs_send, rs_recv))
+    line = Line(count, ATTEND_BLOCKS, [(grad_ref, grad_all)], [(part, land)], (ag_send, ag_recv), (rs_send, rs_recv))
     loads = padded_loads(weight_hbm, last_hbm, weight, last, load_sem)
     line.barrier(wide or 1)
     line.start_own()
@@ -957,20 +868,20 @@
     return turn_tables(length), gains, jnp.transpose(project_weight, (1, 2, 0)), output_weight
 
 
-def line_sems(count, gathers, sums, loads=2):
+def line_sems(count, blocks, gathers, sums, loads=2):
     return [
         pltpu.SemaphoreType.DMA((loads,)),
         pltpu.SemaphoreType.DMA((gathers, 2, count)),
         pltpu.SemaphoreType.DMA((gathers, 2, count)),
-        pltpu.SemaphoreType.DMA((sums, 2, count, CHUNKS)),
-        pltpu.SemaphoreType.DMA((sums, 2, count, CHUNKS)),
+        pltpu.SemaphoreType.DMA((sums, 2, count, blocks)),
+        pltpu.SemaphoreType.DMA((sums, 2, count, blocks)),
     ]
 
 
-def attend_pass(mod_in, arrays):
+def attend_pass(tokens, slabs, arrays):
     count = lax.axis_size("tensor")
     tables, gains, weight, last = arrays
-    item = mod_in.shape
+    item = tokens.shape
     width = item[1]
     heads = last.shape[0] // HD
     inner = heads * LANES
@@ -981,10 +892,13 @@
         out_shape=(
             jax.ShapeDtypeStruct(item, jnp.float32),
             jax.ShapeDtypeStruct((count, *item), low),
+            jax.ShapeDtypeStruct((slabs.shape[1], width), jnp.float32),
         ),
-        in_specs=[vmem, vmem, vmem, any_space, any_space],
-        out_specs=(vmem, vmem),
+        in_specs=[vmem, vmem, vmem, vmem, any_space, any_space],
+        out_specs=(vmem, vmem, vmem),
         scratch_shapes=[
+            pltpu.VMEM(slabs.shape, low),
+            pltpu.VMEM(item, low),
             pltpu.VMEM((3, inner, width), low),
             pltpu.VMEM((inner, width), low),
             pltpu.VMEM((count, *item), low),
@@ -992,13 +906,15 @@
             pltpu.VMEM((item[0], inner), low),
             pltpu.VMEM((count, *item), low),
             pltpu.VMEM((count + 1, *item), low),
-            *line_sems(count, 1, 1, 4 * heads),
+            *line_sems(count, ATTEND_BLOCKS, 1, 1, 4 * heads),
+            pltpu.SemaphoreType.DMA((count,)),
+            pltpu.SemaphoreType.DMA((count,)),
         ],
         compiler_params=pltpu.CompilerParams(
             collective_id=6, has_side_effects=True, vmem_limit_bytes=60000000
         ),
         name="attend_pass",
-    )(mod_in, tables, gains, weight, last)
+    )(tokens, slabs, tables, gains, weight, last)
 
 
 def attend_back_pass(attend_grad, mod_all, arrays, feed_weights):
@@ -1035,7 +951,7 @@
         pltpu.VMEM((count, *item), low),
         pltpu.VMEM((count + 1, *item), low),
         pltpu.VMEM((width, columns), high),
-        *line_sems(count, 1, 1, 4 * heads),
+        *line_sems(count, ATTEND_BLOCKS, 1, 1, 4 * heads),
     ]
     ins = [attend_grad, mod_all, tables, gains, weight, last]
     specs = [vmem, vmem, vmem, vmem, any_space, any_space]
@@ -1214,7 +1130,7 @@
         batch = pl.ds(index * items, items)
         for kind in range(forward_all.shape[0]):
             forward_all[kind, batch, :] = forward_land[index, kind]
-        feat_all[batch, :] = feat_land[index]
+        feat_all[batch, :] = feat_land[index].astype(jnp.float32)
         label_all[batch, :] = label_land[index]
     finish_mine()
     for index in range(wide):
@@ -1280,7 +1196,7 @@
         ((items, width), low),
         ((wide, items, width), low),
         (forward.shape, high),
-        ((wide, items, freq), high),
+        ((wide, items, freq), low),
         ((wide, items, LANES), jnp.int32),
         ((kinds, batch, slab), high),
         ((batch, width), high),
@@ -1331,7 +1247,6 @@
     items = timesteps.shape[0]
     slab = modulate_weight.shape[2]
     heads_here = project_weight.shape[2] // HD
-    scale = HD ** (-0.5)
     first_item = lax.axis_index("tensor") * local_items
     live = (first_item + jnp.arange(local_items) < item_counts[0]).astype(jnp.float32)[
         :, None, None
@@ -1352,17 +1267,13 @@
         jnp.einsum("bd,dke->bke", cond_act, modulate_weight, preferred_element_type=jnp.float32)
         + modulate_bias.astype(jnp.float32)
     ).astype(jnp.bfloat16)
-    (modulation_local,) = swap("modulation_swap", 2, [(modulation_part, "tensor", True)])
-    modulation_local = jnp.transpose(modulation_local, (1, 0, 2)).reshape(1, 6, width)
-    modulation_local = modulation_local.astype(jnp.float32)
-    local_parts = [modulation_local[:, which][:, None, :] for which in range(6)]
-    attend_shift, attend_scale, attend_gate, feed_shift, feed_scale, feed_gate = local_parts
-    positions = jnp.arange(length)
+    arrays = attend_arrays(project_weight, output_weight, query_gain, key_gain, length)
+    attend_total, mod_all, modulation = attend_pass(tokens[0], modulation_part, arrays)
+    _, attend_scale, attend_gate, feed_shift, feed_scale, feed_gate = [
+        modulation[which][None, None, :] for which in range(6)
+    ]
     token_local = tokens.astype(jnp.float32)
     normed_local, inverse_local = layer_norm(token_local)
-    mod_in = normed_local * (1.0 + attend_scale) + attend_shift
-    arrays = attend_arrays(project_weight, output_weight, query_gain, key_gain, length)
-    attend_total, mod_all = attend_pass(mod_in[0].astype(jnp.bfloat16), arrays)
     attend_branch = attend_total[None] + output_bias.astype(jnp.float32)
     residual = token_local + attend_gate * attend_branch
     normed_two, inverse_two = layer_norm(residual)
@@ -1402,17 +1313,17 @@
         axis=1,
     )
     modulation_grad_part = modulation_grad_part[0].astype(jnp.bfloat16)
+    gain_row = jnp.pad(
+        jnp.concatenate([query_gain_part, key_gain_part])[None], ((0, 0), (0, width - 2 * HD))
+    )
     small = jnp.concatenate(
         [
-            output_bias_part,
-            down_bias_part,
-            modulation_grad_part.astype(jnp.float32).reshape(-1),
-            query_gain_part,
-            key_gain_part,
+            output_bias_part[None],
+            down_bias_part[None],
+            modulation_grad_part.astype(jnp.float32),
+            gain_row,
         ]
     )
-    small_size = small.shape[0]
-    small = jnp.pad(small, (0, -small_size % 1024)).reshape(-1, 128)
     tensor_size, wide = width // slab, lax.axis_size("dp")
     share = width // wide
 
@@ -1428,7 +1339,7 @@
         jnp.transpose(modulate_weight, (1, 2, 0)),
         silu_slope(condition),
         jnp.stack([shares(cond_act), shares(time_hidden), shares(silu_slope(pre_hidden))], axis=1),
-        time_feat.astype(jnp.float32),
+        time_feat,
         jnp.broadcast_to(labels[:, None], (items, LANES)),
         rows,
         class_table.shape[0],
@@ -1436,12 +1347,9 @@
     class_grad, time_grad = class_grad.T, time_grad.T
     modulate_grad = jnp.transpose(modulate_grad, (1, 0, 2))
     embed_bias_grad, time_bias_grad = biases
-    small = small.reshape(-1)
-    output_bias_grad = small[:width]
-    down_bias_grad = small[width : 2 * width]
-    modulate_bias_grad = small[2 * width : 8 * width].reshape(6, width)
-    query_gain_grad = small[8 * width : 8 * width + HD]
-    key_gain_grad = small[8 * width + HD : 8 * width + 2 * HD]
+    output_bias_grad, down_bias_grad = small[0], small[1]
+    modulate_bias_grad = small[2:8]
+    query_gain_grad, key_gain_grad = small[8, :HD], small[8, HD : 2 * HD]
     inner = heads_here * HD
     first_width = attend_weights.shape[1] - -(-inner // LANES) * LANES
     project_grad = attend_weights[:, : 3 * inner].reshape(-1, 3, inner)

time: 367 us -> 368 us (level)
    pallas_call x1 -> x0, Pallas kernels: 8.72 us -> none  [swap(): pl.pallas_call(functools.partial(swap_kernel, tuple(plan), int(total is n...]
    pallas_call x1, Pallas kernels: 113 us -> 119 us  [feed_pass(): pl.pallas_call(functools.partial(feed_kernel, count), out_shape=(jax.Shap...]
    pallas_call x1, Pallas kernels: 76.9 us -> 81.7 us  [attend_pass(): pl.pallas_call(functools.partial(attend_kernel, count), out_shape=(jax.Sh...]
    unnamed x53 -> x59, local copies, waits for them, and re-layouts: 13.2 us -> 13.1 us
where the time goes in v2:
time: 368 us; the launch traced here: 366 us
  Pallas kernels  311 us (85%)
  local copies, waits for them, and re-layouts  26.4 us (7%)
  other arithmetic  19.8 us (5%)
  matrix products  6.54 us (2%)
    pallas_call x1, Pallas kernels, feed_pass(): pl.pallas_call(functools.partial(feed_kernel, count), out_shape=(jax.Shap...  119 us
    pallas_call x1, Pallas kernels, attend_back_pass(): pl.pallas_call(functools.partial(attend_back_kernel, count, wide), out_sh...  89.7 us
    pallas_call x1, Pallas kernels, attend_pass(): pl.pallas_call(functools.partial(attend_kernel, count), out_shape=(jax.Sh...  81.7 us
    pallas_call x1, Pallas kernels, tail_pass(): pl.pallas_call(tail_kernel, out_shape=tuple((jax.ShapeDtypeStruct(*shape)...  21.3 us
    unnamed x59, local copies, waits for them, and re-layouts  13.1 us

profile of v2, /device:TPU:0, one launch (start us, length us, event | category | flops | bytes accessed | tf_op | source)
XLA Modules:
  0.0 365.9 jit_solution(1147263553632821119)
XLA Ops:
  1.3 0.8 pad_maximum_fusion.tables_ref
  2.5 2.5 gather_fusion
  5.1 2.8 fusion.46
  7.9 3.5 fusion.27
  12.7 81.7 %attend_pass.1 = (f32[256,1152]{1,0:T(8,128)}, bf16[4,256,1152]{2,1,0:T(8,128)(2,1)}, f32[6,1152]{1,0:T(8,128)}) custom-call(bf16[256,1152]{1,0:T(8,128)(2,1)} %bitcast.100, bf16[4,6,288]{2,1,0:T(8,128)(2,1)} %fusion.26.slab_ref, f32[3,256,128]{2,1,0:T(8,128)} %pad_maximum_fusion.tables_ref, f32[8,128]{1,0:T(8,128)} %fusion.37.gains_ref, ...), custom_call_target="tpu_custom_call" | custom-call | tf_op jit(solution)/shard_map/attend_pass/pallas_call | solution.py:890
  94.3 1.1 add_reduce_fusion
  95.6 1.7 fusion.50
  97.6 1.1 fusion.21.mod_ref
  99.4 1.0 fusion.22.grad_ref
  100.4 4.3 %copy.61 = bf16[1152,2,768]{2,0,1:T(8,128)(2,1)} copy(bf16[1152,2,768]{2,1,0:T(2,128)(2,1)} %param.30) | data formatting | bytes 7077888 | tf_op args[10]
  104.6 118.7 %feed_pass.1 = (f32[256,1152]{1,0:T(8,128)}, f32[256,1152]{1,0:T(8,128)}, bf16[3,1152,768]{2,1,0:T(8,128)(2,1)}) custom-call(bf16[256,1152]{1,0:T(8,128)(2,1)} %fusion.21.mod_ref, bf16[256,1152]{1,0:T(8,128)(2,1)} %fusion.22.grad_ref, bf16[2,1152,768]{2,1,0:T(8,128)(2,1)} %bitcast.101, bf16[768,1152]{1,0:T(8,128)(2,1)} %down_hbm.1), custom_call_target="tpu_custom_call" | custom-call | tf_op jit(solution)/shard_map/feed_pass/pallas_call | solution.py:394
  223.4 1.6 fusion.47
  226.7 2.2 convert_reduce_fusion.1
  228.9 1.0 copy-done.5
  229.9 0.9 fusion.23.grad_ref
  230.8 89.7 %attend_back_pass.1 = (f32[256,1152]{1,0:T(8,128)}, f32[144,1280]{1,0:T(8,128)}, f32[2,8,128]{2,1,0:T(8,128)}, f32[3,144,768]{2,1,0:T(8,128)}) custom-call(bf16[256,1152]{1,0:T(8,128)(2,1)} %fusion.23.grad_ref, bf16[4,256,1152]{2,1,0:T(8,128)(2,1)} %get-tuple-element.37.mod_all, f32[3,256,128]{2,1,0:T(8,128)} %pad_maximum_fusion.tables_ref, ...), custom_call_target="tpu_custom_call" | custom-call | tf_op jit(solution)/shard_map/attend_back_pass/pallas_call | solution.py:972
  320.5 1.5 fusion.48
  322.1 1.8 fusion.11
  325.3 0.7 stack.85
  328.2 21.3 %tail_pass.1 = (f32[9,1152]{1,0:T(8,128)}, f32[6,144,288]{2,1,0:T(8,128)}, f32[144,1152]{1,0:T(8,128)}, f32[144,1000]{1,0:T(8,128)}, f32[144,256]{1,0:T(8,128)}, /*index=5*/f32[2,144]{1,0:T(2,128)}) custom-call(bf16[4,6,288]{2,1,0:T(8,128)(2,1)} %bitcast.108, f32[9,1152]{1,0:T(8,128)} %select_maximum_fusion.small_ref, bf16[6,288,1152]{2,1,0:T(8,128)(2,1)} %bitcast.99, ...), custom_call_target="tpu_custom_call" | custom-call | tf_op jit(solution)/shard_map/tail_pass/pallas_call | solution.py:1211
  349.5 1.4 slice.58
  350.9 1.5 slice_reduce_fusion
  352.4 1.3 fusion.51
  353.7 1.3 slice_bitcast_fusion.3
  355.5 0.9 copy.52
  357.2 1.6 copy.53
  358.8 1.3 fusion.10
  360.0 0.8 slice_bitcast_fusion.1
  360.8 1.6 slice_bitcast_fusion.2
  362.5 1.1 copy.68
  364.2 0.8 copy.70
  365.1 0.8 copy.71
  (112 shorter events, 9.9 us)
Async XLA Ops:
  0.7 1.6 copy-start
  0.7 1.5 copy-start.25
  0.7 1.6 copy-start.18
  0.7 1.8 copy-start.24
  0.7 4.4 %copy-start.19 = (bf16[1152]{0:T(1024)(128)(2,1)S(1)}, bf16[1152]{0:T(1024)(128)(2,1)}, u32[]{:S(2)}) copy-start(bf16[1152]{0:T(1024)(128)(2,1)} %param.38) | copy-start | bytes 6916
  7.9 3.5 copy-start.17
  7.9 4.1 %copy-start.22 = (bf16[72]{0:T(256)(128)(2,1)S(1)}, bf16[72]{0:T(256)(128)(2,1)}, u32[]{:S(2)}) copy-start(bf16[72]{0:T(256)(128)(2,1)} %param.27) | copy-start | bytes 436
  7.9 4.1 %copy-start.23 = (bf16[72]{0:T(256)(128)(2,1)S(1)}, bf16[72]{0:T(256)(128)(2,1)}, u32[]{:S(2)}) copy-start(bf16[72]{0:T(256)(128)(2,1)} %param.26) | copy-start | bytes 436
  12.7 82.7 %copy-start.1 = (bf16[1,256,1152]{2,1,0:T(8,128)(2,1)S(1)}, bf16[1,256,1152]{2,1,0:T(8,128)(2,1)}, u32[]{:S(2)}) copy-start(bf16[1,256,1152]{2,1,0:T(8,128)(2,1)} %param.20) | copy-start | bytes 1769476
  12.7 82.9 %copy-start.20 = (bf16[1152]{0:T(1024)(128)(2,1)S(1)}, bf16[1152]{0:T(1024)(128)(2,1)}, u32[]{:S(2)}) copy-start(bf16[1152]{0:T(1024)(128)(2,1)} %param.29) | copy-start | bytes 6916
  97.6 1.8 copy-start.8
  223.4 1.6 copy-start.4
  225.0 0.7 copy-start.21
  225.0 1.3 copy-start.7
  225.0 1.6 copy-start.11
  228.9 1.0 copy-start.5
  320.5 1.6 copy-start.2
  322.1 1.9 copy-start.16
  328.2 26.8 %copy-start.12 = (f32[144,1280]{1,0:T(8,128)S(1)}, f32[144,1280]{1,0:T(8,128)}, u32[]{:S(2)}) copy-start(f32[144,1280]{1,0:T(8,128)} %get-tuple-element.40) | copy-start | bytes 2211844
  355.5 1.6 copy-start.9
  357.1 1.7 copy-start.6
  357.1 1.6 copy-start.3
  360.0 2.4 copy-start.10
  362.5 1.1 copy-start.15
  362.5 1.7 copy-start.13
  363.5 1.5 copy-start.14

commit v3 on v2

--- a/solution.py
+++ b/solution.py
@@ -135,9 +135,9 @@
                 def _():
                     self.item_copy(which, way, self.place, own=True).start()
 
-    def receive(self, step):
+    def receive(self, step, arrays=(0,)):
         place, count = self.place, self.count
-        for which in range(len(self.gathered)):
+        for which in arrays:
             for way in range(2):
                 item = place - step if way == 0 else place + step
 
@@ -293,6 +293,7 @@
     back_land,
     total,
     weights,
+    gates,
     load_sem,
     ag_send,
     ag_recv,
@@ -325,21 +326,33 @@
     wide_size, wide_count = cut(width, 384)
     tall_size, tall_count = cut(width, 128)
 
-    def compute(item):
+    def ahead(item):
         @pl.loop(0, unit_count)
         def _(index):
             cols = span(index, unit_size)
             mod = mod_all[item]
             gate = dot(mod, expand[0, :, cols])
             upper = dot(mod, expand[1, :, cols])
+            gates[0, item, :, cols] = gate
+            gates[1, item, :, cols] = upper
+            hidden[item, :, cols] = (gate * jax.nn.sigmoid(gate) * upper).astype(jnp.bfloat16)
+
+        @pl.loop(0, wide_count)
+        def _(index):
+            cols = span(index, wide_size)
+            feed_part[item, :, cols] = dot(hidden[item], down[:, cols]).astype(jnp.bfloat16)
+
+    def behind(item):
+        @pl.loop(0, unit_count)
+        def _(index):
+            cols = span(index, unit_size)
             back = dot_rt(grad_all[item], down[cols, :])
+            gate = gates[0, item, :, cols]
             sigma = jax.nn.sigmoid(gate)
-            active = gate * sigma
-            hidden[item, :, cols] = (active * upper).astype(jnp.bfloat16)
             slopes[0, item, :, cols] = (
-                back * upper * (sigma * (1.0 + gate * (1.0 - sigma)))
+                back * gates[1, item, :, cols] * (sigma * (1.0 + gate * (1.0 - sigma)))
             ).astype(jnp.bfloat16)
-            slopes[1, item, :, cols] = (back * active).astype(jnp.bfloat16)
+            slopes[1, item, :, cols] = (back * (gate * sigma)).astype(jnp.bfloat16)
 
         @pl.loop(0, wide_count)
         def _(index):
@@ -348,7 +361,6 @@
                 dot_rt(slopes[0, item], expand[0, cols, :])
                 + dot_rt(slopes[1, item], expand[1, cols, :])
             ).astype(jnp.bfloat16)
-            feed_part[item, :, cols] = dot(hidden[item], down[:, cols]).astype(jnp.bfloat16)
 
     def weigh(item):
         @pl.loop(0, tall_count)
@@ -364,21 +376,29 @@
         @pl.when(step > 0)
         def _():
             line.each(line.far(step - 1), line.near(step - 1), weigh)
-            line.receive(step)
-
-        line.each(line.far(step), line.near(step), compute)
+            line.receive(step, (0,))
+
+        line.each(line.far(step), line.near(step), ahead)
 
         @pl.when(step > 0)
         def _():
-            line.first_sums(step, (0, 1))
-            line.relay_sums(step, (0, 1))
+            line.first_sums(step, (1,))
+            line.receive(step, (1,))
+
+        line.each(line.far(step), line.near(step), behind)
+
+        @pl.when(step > 0)
+        def _():
+            line.first_sums(step, (0,))
+            line.relay_sums(step, (1,))
+            line.relay_sums(step, (0,))
 
     line.each((0, False), line.near(count - 1), weigh)
     weights[...] = total[...].astype(jnp.bfloat16)
     store = pltpu.make_async_copy(weights, weight_hbm, load_sem.at[0])
     store.start()
+    line.finish(1, feed_out)
     line.finish(0, back_out)
-    line.finish(1, feed_out)
     line.drain()
     store.wait()
 
@@ -413,6 +433,7 @@
             pltpu.VMEM((count + 1, *item), low),
             pltpu.VMEM((3, width, units), jnp.float32),
             pltpu.VMEM((3, width, units), low),
+            pltpu.VMEM((2, count, length, units), jnp.float32),
             *line_sems(count, FEED_BLOCKS, 2, 2),
         ],
         compiler_params=pltpu.CompilerParams(
@@ -1313,17 +1334,17 @@
         axis=1,
     )
     modulation_grad_part = modulation_grad_part[0].astype(jnp.bfloat16)
-    gain_row = jnp.pad(
-        jnp.concatenate([query_gain_part, key_gain_part])[None], ((0, 0), (0, width - 2 * HD))
-    )
     small = jnp.concatenate(
         [
-            output_bias_part[None],
-            down_bias_part[None],
-            modulation_grad_part.astype(jnp.float32),
-            gain_row,
+            output_bias_part,
+            down_bias_part,
+            modulation_grad_part.astype(jnp.float32).reshape(-1),
+            query_gain_part,
+            key_gain_part,
         ]
     )
+    small_size = small.shape[0]
+    small = jnp.pad(small, (0, -small_size % 1024)).reshape(-1, 128)
     tensor_size, wide = width // slab, lax.axis_size("dp")
     share = width // wide
 
@@ -1347,9 +1368,12 @@
     class_grad, time_grad = class_grad.T, time_grad.T
     modulate_grad = jnp.transpose(modulate_grad, (1, 0, 2))
     embed_bias_grad, time_bias_grad = biases
-    output_bias_grad, down_bias_grad = small[0], small[1]
-    modulate_bias_grad = small[2:8]
-    query_gain_grad, key_gain_grad = small[8, :HD], small[8, HD : 2 * HD]
+    small = small.reshape(-1)
+    output_bias_grad = small[:width]
+    down_bias_grad = small[width : 2 * width]
+    modulate_bias_grad = small[2 * width : 8 * width].reshape(6, width)
+    query_gain_grad = small[8 * width : 8 * width + HD]
+    key_gain_grad = small[8 * width + HD : 8 * width + 2 * HD]
     inner = heads_here * HD
     first_width = attend_weights.shape[1] - -(-inner // LANES) * LANES
     project_grad = attend_weights[:, : 3 * inner].reshape(-1, 3, inner)

time: 368 us -> 368 us (level)
    pallas_call x1, Pallas kernels: 119 us -> 125 us  [feed_pass(): pl.pallas_call(functools.partial(feed_kernel, count), out_shape=(jax.Shap...]
where the time goes in v3:
time: 368 us; the launch traced here: 367 us
  Pallas kernels  314 us (85%)
  local copies, waits for them, and re-layouts  26.1 us (7%)
  other arithmetic  19 us (5%)
  matrix products  6.54 us (2%)
    pallas_call x1, Pallas kernels, feed_pass(): pl.pallas_call(functools.partial(feed_kernel, count), out_shape=(jax.Shap...  125 us
    pallas_call x1, Pallas kernels, attend_back_pass(): pl.pallas_call(functools.partial(attend_back_kernel, count, wide), out_sh...  88.6 us
    pallas_call x1, Pallas kernels, attend_pass(): pl.pallas_call(functools.partial(attend_kernel, count), out_shape=(jax.Sh...  81.7 us
    pallas_call x1, Pallas kernels, tail_pass(): pl.pallas_call(tail_kernel, out_shape=tuple((jax.ShapeDtypeStruct(*shape)...  18.8 us
    unnamed x59, local copies, waits for them, and re-layouts  13.1 us

profile of v3, /device:TPU:0, one launch (start us, length us, event | category | flops | bytes accessed | tf_op | source)
XLA Modules:
  0.0 367.1 jit_solution(15967841508964657242)
XLA Ops:
  1.3 0.8 pad_maximum_fusion.tables_ref
  2.5 2.5 gather_fusion
  5.1 2.8 fusion.46
  7.9 3.5 fusion.27
  12.7 81.7 %attend_pass.1 = (f32[256,1152]{1,0:T(8,128)}, bf16[4,256,1152]{2,1,0:T(8,128)(2,1)}, f32[6,1152]{1,0:T(8,128)}) custom-call(bf16[256,1152]{1,0:T(8,128)(2,1)} %bitcast.99, bf16[4,6,288]{2,1,0:T(8,128)(2,1)} %fusion.26.slab_ref, f32[3,256,128]{2,1,0:T(8,128)} %pad_maximum_fusion.tables_ref, f32[8,128]{1,0:T(8,128)} %fusion.37.gains_ref, ...), custom_call_target="tpu_custom_call" | custom-call | tf_op jit(solution)/shard_map/attend_pass/pallas_call | solution.py:911
  94.3 1.1 add_reduce_fusion
  95.6 1.7 fusion.50
  97.6 1.1 fusion.21.mod_ref
  99.4 1.0 fusion.22.grad_ref
  100.4 4.3 %copy.61 = bf16[1152,2,768]{2,0,1:T(8,128)(2,1)} copy(bf16[1152,2,768]{2,1,0:T(2,128)(2,1)} %param.30) | data formatting | bytes 7077888 | tf_op args[10]
  104.6 124.7 %feed_pass.1 = (f32[256,1152]{1,0:T(8,128)}, f32[256,1152]{1,0:T(8,128)}, bf16[3,1152,768]{2,1,0:T(8,128)(2,1)}) custom-call(bf16[256,1152]{1,0:T(8,128)(2,1)} %fusion.21.mod_ref, bf16[256,1152]{1,0:T(8,128)(2,1)} %fusion.22.grad_ref, bf16[2,1152,768]{2,1,0:T(8,128)(2,1)} %bitcast.100, bf16[768,1152]{1,0:T(8,128)(2,1)} %down_hbm.1), custom_call_target="tpu_custom_call" | custom-call | tf_op jit(solution)/shard_map/feed_pass/pallas_call | solution.py:414
  229.3 1.6 fusion.47
  232.6 2.2 convert_reduce_fusion.1
  234.8 1.0 copy-done.5
  235.8 0.9 fusion.23.grad_ref
  236.7 88.6 %attend_back_pass.1 = (f32[256,1152]{1,0:T(8,128)}, f32[144,1280]{1,0:T(8,128)}, f32[2,8,128]{2,1,0:T(8,128)}, f32[3,144,768]{2,1,0:T(8,128)}) custom-call(bf16[256,1152]{1,0:T(8,128)(2,1)} %fusion.23.grad_ref, bf16[4,256,1152]{2,1,0:T(8,128)(2,1)} %get-tuple-element.37.mod_all, f32[3,256,128]{2,1,0:T(8,128)} %pad_maximum_fusion.tables_ref, ...), custom_call_target="tpu_custom_call" | custom-call | tf_op jit(solution)/shard_map/attend_back_pass/pallas_call | solution.py:993
  325.3 1.5 fusion.48
  326.9 1.8 fusion.11
  330.1 0.7 stack.85
  333.0 18.8 %tail_pass.1 = (f32[80,128]{1,0:T(8,128)}, f32[6,144,288]{2,1,0:T(8,128)}, f32[144,1152]{1,0:T(8,128)}, f32[144,1000]{1,0:T(8,128)}, f32[144,256]{1,0:T(8,128)}, /*index=5*/f32[2,144]{1,0:T(2,128)}) custom-call(bf16[4,6,288]{2,1,0:T(8,128)(2,1)} %bitcast.107, f32[80,128]{1,0:T(8,128)} %pad_bitcast_fusion.small_ref, bf16[6,288,1152]{2,1,0:T(8,128)(2,1)} %bitcast.98, ...), custom_call_target="tpu_custom_call" | custom-call | tf_op jit(solution)/shard_map/tail_pass/pallas_call | solution.py:1232
  351.8 0.8 slice.67
  353.2 1.4 slice_bitcast_fusion.3
  354.6 1.3 fusion.52
  355.9 1.3 fusion.51
  357.7 0.9 copy.52
  359.4 1.6 copy.53
  361.0 1.3 fusion.10
  362.3 0.8 slice_bitcast_fusion.1
  363.1 0.7 slice_bitcast_fusion.2
  363.8 1.1 copy.68
  365.5 0.8 copy.70
  366.3 0.8 copy.71
  (111 shorter events, 10.5 us)
Async XLA Ops:
  0.7 1.6 copy-start
  0.7 1.5 copy-start.25
  0.7 1.6 copy-start.18
  0.7 1.8 copy-start.24
  0.7 4.4 %copy-start.19 = (bf16[1152]{0:T(1024)(128)(2,1)S(1)}, bf16[1152]{0:T(1024)(128)(2,1)}, u32[]{:S(2)}) copy-start(bf16[1152]{0:T(1024)(128)(2,1)} %param.38) | copy-start | bytes 6916
  7.9 3.5 copy-start.17
  7.9 4.1 %copy-start.22 = (bf16[72]{0:T(256)(128)(2,1)S(1)}, bf16[72]{0:T(256)(128)(2,1)}, u32[]{:S(2)}) copy-start(bf16[72]{0:T(256)(128)(2,1)} %param.27) | copy-start | bytes 436
  7.9 4.1 %copy-start.23 = (bf16[72]{0:T(256)(128)(2,1)S(1)}, bf16[72]{0:T(256)(128)(2,1)}, u32[]{:S(2)}) copy-start(bf16[72]{0:T(256)(128)(2,1)} %param.26) | copy-start | bytes 436
  12.7 82.7 %copy-start.1 = (bf16[1,256,1152]{2,1,0:T(8,128)(2,1)S(1)}, bf16[1,256,1152]{2,1,0:T(8,128)(2,1)}, u32[]{:S(2)}) copy-start(bf16[1,256,1152]{2,1,0:T(8,128)(2,1)} %param.20) | copy-start | bytes 1769476
  12.7 82.9 %copy-start.20 = (bf16[1152]{0:T(1024)(128)(2,1)S(1)}, bf16[1152]{0:T(1024)(128)(2,1)}, u32[]{:S(2)}) copy-start(bf16[1152]{0:T(1024)(128)(2,1)} %param.29) | copy-start | bytes 6916
  97.6 1.8 copy-start.8
  229.3 1.6 copy-start.4
  231.0 0.7 copy-start.21
  231.0 1.3 copy-start.7
  231.0 1.6 copy-start.11
  234.8 1.0 copy-start.5
  325.3 1.6 copy-start.2
  326.9 2.0 copy-start.16
  333.0 24.2 %copy-start.12 = (f32[144,1280]{1,0:T(8,128)S(1)}, f32[144,1280]{1,0:T(8,128)}, u32[]{:S(2)}) copy-start(f32[144,1280]{1,0:T(8,128)} %get-tuple-element.40) | copy-start | bytes 2211844
  357.7 1.6 copy-start.9
  359.3 1.7 copy-start.6
  359.4 1.6 copy-start.3
  362.3 1.5 copy-start.10
  363.8 1.1 copy-start.15
  363.8 1.7 copy-start.13
  364.8 1.5 copy-start.14

commit v4 on v2

--- a/solution.py
+++ b/solution.py
@@ -1313,17 +1313,17 @@
         axis=1,
     )
     modulation_grad_part = modulation_grad_part[0].astype(jnp.bfloat16)
-    gain_row = jnp.pad(
-        jnp.concatenate([query_gain_part, key_gain_part])[None], ((0, 0), (0, width - 2 * HD))
-    )
     small = jnp.concatenate(
         [
-            output_bias_part[None],
-            down_bias_part[None],
-            modulation_grad_part.astype(jnp.float32),
-            gain_row,
+            output_bias_part,
+            down_bias_part,
+            modulation_grad_part.astype(jnp.float32).reshape(-1),
+            query_gain_part,
+            key_gain_part,
         ]
     )
+    small_size = small.shape[0]
+    small = jnp.pad(small, (0, -small_size % 1024)).reshape(-1, 128)
     tensor_size, wide = width // slab, lax.axis_size("dp")
     share = width // wide
 
@@ -1347,9 +1347,12 @@
     class_grad, time_grad = class_grad.T, time_grad.T
     modulate_grad = jnp.transpose(modulate_grad, (1, 0, 2))
     embed_bias_grad, time_bias_grad = biases
-    output_bias_grad, down_bias_grad = small[0], small[1]
-    modulate_bias_grad = small[2:8]
-    query_gain_grad, key_gain_grad = small[8, :HD], small[8, HD : 2 * HD]
+    small = small.reshape(-1)
+    output_bias_grad = small[:width]
+    down_bias_grad = small[width : 2 * width]
+    modulate_bias_grad = small[2 * width : 8 * width].reshape(6, width)
+    query_gain_grad = small[8 * width : 8 * width + HD]
+    key_gain_grad = small[8 * width + HD : 8 * width + 2 * HD]
     inner = heads_here * HD
     first_width = attend_weights.shape[1] - -(-inner // LANES) * LANES
     project_grad = attend_weights[:, : 3 * inner].reshape(-1, 3, inner)

time: 368 us -> 363 us (0.986)
  no operation moved by 1% of the time
where the time goes in v4:
time: 363 us; the launch traced here: 362 us
  Pallas kernels  308 us (85%)
  local copies, waits for them, and re-layouts  26.1 us (7%)
  other arithmetic  19 us (5%)
  matrix products  6.54 us (2%)
    pallas_call x1, Pallas kernels, feed_pass(): pl.pallas_call(functools.partial(feed_kernel, count), out_shape=(jax.Shap...  119 us
    pallas_call x1, Pallas kernels, attend_back_pass(): pl.pallas_call(functools.partial(attend_back_kernel, count, wide), out_sh...  89.8 us
    pallas_call x1, Pallas kernels, attend_pass(): pl.pallas_call(functools.partial(attend_kernel, count), out_shape=(jax.Sh...  81.7 us
    pallas_call x1, Pallas kernels, tail_pass(): pl.pallas_call(tail_kernel, out_shape=tuple((jax.ShapeDtypeStruct(*shape)...  18.3 us
    unnamed x59, local copies, waits for them, and re-layouts  13.1 us

profile of v4, /device:TPU:0, one launch (start us, length us, event | category | flops | bytes accessed | tf_op | source)
XLA Modules:
  0.0 361.8 jit_solution(12378758848836065204)
XLA Ops:
  1.3 0.8 pad_maximum_fusion.tables_ref
  2.5 2.5 gather_fusion
  5.1 2.8 fusion.46
  7.9 3.5 fusion.27
  12.7 81.7 %attend_pass.1 = (f32[256,1152]{1,0:T(8,128)}, bf16[4,256,1152]{2,1,0:T(8,128)(2,1)}, f32[6,1152]{1,0:T(8,128)}) custom-call(bf16[256,1152]{1,0:T(8,128)(2,1)} %bitcast.99, bf16[4,6,288]{2,1,0:T(8,128)(2,1)} %fusion.26.slab_ref, f32[3,256,128]{2,1,0:T(8,128)} %pad_maximum_fusion.tables_ref, f32[8,128]{1,0:T(8,128)} %fusion.37.gains_ref, ...), custom_call_target="tpu_custom_call" | custom-call | tf_op jit(solution)/shard_map/attend_pass/pallas_call | solution.py:890
  94.3 1.1 add_reduce_fusion
  95.6 1.7 fusion.50
  97.6 1.1 fusion.21.mod_ref
  99.4 1.0 fusion.22.grad_ref
  100.4 4.3 %copy.61 = bf16[1152,2,768]{2,0,1:T(8,128)(2,1)} copy(bf16[1152,2,768]{2,1,0:T(2,128)(2,1)} %param.30) | data formatting | bytes 7077888 | tf_op args[10]
  104.6 118.7 %feed_pass.1 = (f32[256,1152]{1,0:T(8,128)}, f32[256,1152]{1,0:T(8,128)}, bf16[3,1152,768]{2,1,0:T(8,128)(2,1)}) custom-call(bf16[256,1152]{1,0:T(8,128)(2,1)} %fusion.21.mod_ref, bf16[256,1152]{1,0:T(8,128)(2,1)} %fusion.22.grad_ref, bf16[2,1152,768]{2,1,0:T(8,128)(2,1)} %bitcast.100, bf16[768,1152]{1,0:T(8,128)(2,1)} %down_hbm.1), custom_call_target="tpu_custom_call" | custom-call | tf_op jit(solution)/shard_map/feed_pass/pallas_call | solution.py:394
  223.3 1.6 fusion.47
  226.6 2.2 convert_reduce_fusion.1
  228.8 1.0 copy-done.5
  229.8 0.9 fusion.23.grad_ref
  230.7 89.8 %attend_back_pass.1 = (f32[256,1152]{1,0:T(8,128)}, f32[144,1280]{1,0:T(8,128)}, f32[2,8,128]{2,1,0:T(8,128)}, f32[3,144,768]{2,1,0:T(8,128)}) custom-call(bf16[256,1152]{1,0:T(8,128)(2,1)} %fusion.23.grad_ref, bf16[4,256,1152]{2,1,0:T(8,128)(2,1)} %get-tuple-element.37.mod_all, f32[3,256,128]{2,1,0:T(8,128)} %pad_maximum_fusion.tables_ref, ...), custom_call_target="tpu_custom_call" | custom-call | tf_op jit(solution)/shard_map/attend_back_pass/pallas_call | solution.py:972
  320.5 1.5 fusion.48
  322.1 1.8 fusion.11
  325.3 0.7 stack.85
  328.2 18.3 %tail_pass.1 = (f32[80,128]{1,0:T(8,128)}, f32[6,144,288]{2,1,0:T(8,128)}, f32[144,1152]{1,0:T(8,128)}, f32[144,1000]{1,0:T(8,128)}, f32[144,256]{1,0:T(8,128)}, /*index=5*/f32[2,144]{1,0:T(2,128)}) custom-call(bf16[4,6,288]{2,1,0:T(8,128)(2,1)} %bitcast.107, f32[80,128]{1,0:T(8,128)} %pad_bitcast_fusion.small_ref, bf16[6,288,1152]{2,1,0:T(8,128)(2,1)} %bitcast.98, ...), custom_call_target="tpu_custom_call" | custom-call | tf_op jit(solution)/shard_map/tail_pass/pallas_call | solution.py:1211
  346.5 0.8 slice.67
  347.9 1.4 slice_bitcast_fusion.3
  349.3 1.3 fusion.52
  350.6 1.3 fusion.51
  352.4 0.9 copy.52
  354.1 1.6 copy.53
  355.7 1.3 fusion.10
  357.0 0.8 slice_bitcast_fusion.1
  357.7 0.7 slice_bitcast_fusion.2
  358.5 1.1 copy.68
  360.2 0.8 copy.70
  361.0 0.8 copy.71
  (111 shorter events, 10.5 us)
Async XLA Ops:
  0.7 1.6 copy-start
  0.7 1.5 copy-start.25
  0.7 1.6 copy-start.18
  0.7 1.8 copy-start.24
  0.7 4.4 %copy-start.19 = (bf16[1152]{0:T(1024)(128)(2,1)S(1)}, bf16[1152]{0:T(1024)(128)(2,1)}, u32[]{:S(2)}) copy-start(bf16[1152]{0:T(1024)(128)(2,1)} %param.38) | copy-start | bytes 6916
  7.9 3.5 copy-start.17
  7.9 4.1 %copy-start.22 = (bf16[72]{0:T(256)(128)(2,1)S(1)}, bf16[72]{0:T(256)(128)(2,1)}, u32[]{:S(2)}) copy-start(bf16[72]{0:T(256)(128)(2,1)} %param.27) | copy-start | bytes 436
  7.9 4.1 %copy-start.23 = (bf16[72]{0:T(256)(128)(2,1)S(1)}, bf16[72]{0:T(256)(128)(2,1)}, u32[]{:S(2)}) copy-start(bf16[72]{0:T(256)(128)(2,1)} %param.26) | copy-start | bytes 436
  12.7 82.7 %copy-start.1 = (bf16[1,256,1152]{2,1,0:T(8,128)(2,1)S(1)}, bf16[1,256,1152]{2,1,0:T(8,128)(2,1)}, u32[]{:S(2)}) copy-start(bf16[1,256,1152]{2,1,0:T(8,128)(2,1)} %param.20) | copy-start | bytes 1769476
  12.7 82.9 %copy-start.20 = (bf16[1152]{0:T(1024)(128)(2,1)S(1)}, bf16[1152]{0:T(1024)(128)(2,1)}, u32[]{:S(2)}) copy-start(bf16[1152]{0:T(1024)(128)(2,1)} %param.29) | copy-start | bytes 6916
  97.6 1.8 copy-start.8
  223.3 1.6 copy-start.4
  224.9 0.7 copy-start.21
  224.9 1.3 copy-start.7
  224.9 1.6 copy-start.11
  228.8 1.0 copy-start.5
  320.5 1.6 copy-start.2
  322.1 2.0 copy-start.16
  328.2 23.7 %copy-start.12 = (f32[144,1280]{1,0:T(8,128)S(1)}, f32[144,1280]{1,0:T(8,128)}, u32[]{:S(2)}) copy-start(f32[144,1280]{1,0:T(8,128)} %get-tuple-element.40) | copy-start | bytes 2211844
  352.4 1.6 copy-start.9
  354.0 1.7 copy-start.6
  354.0 1.6 copy-start.3
  357.0 1.5 copy-start.10
  358.4 1.1 copy-start.15
  358.5 1.7 copy-start.13
  359.5 1.5 copy-start.14
